TPU v7x, 64 devices: a 2x2x8 block of a 4x4x8 slice. The times are simulated.
64 devices in a mesh: dp: 4 (over x, y), ep: 16 (over z, core).
Axes of the slice: x: 2, y: 2, z: 8, core: 2. Of those that a mesh axis runs over, the one named last changes fastest.
The devices are a block of a 4x4x8 slice.
Arguments:
- tokens: bfloat16 [64, 512, 1024], P(('dp', 'ep')), parts along dimension 0
- w_query: bfloat16 [1024, 16, 64], P('ep')
- w_key: bfloat16 [1024, 16, 64], P('ep')
- w_value: bfloat16 [1024, 16, 64], P('ep')
- w_out: bfloat16 [1024, 1024], P('ep')
- w_router: float32 [1024, 32], replicated
- w_one: bfloat16 [32, 1024, 512], P('ep')
- w_three: bfloat16 [32, 1024, 512], P('ep')
- w_two: bfloat16 [32, 512, 1024], P('ep')
- expert_ids: int32 [64, 512, 8], P(('dp', 'ep')), parts along dimension 0
Outputs:
- output: bfloat16 [64, 512, 1024], P(('dp', 'ep')), parts along dimension 0
There are 4 independent parts. A program takes and returns all parts, laid end to end along the dimension named above; an argument that names none is the same for every part.
All inputs are finite; a program needn't handle non-finite values.
Results may differ from a plain program's by a relative error of at most 0.00981771.
Values are sent between devices in bfloat16 or wider.
A program may use at most 768 MiB of HBM per device.

v0:
```python
import jax
import jax.numpy as jnp
from jax import lax
from jax.sharding import PartitionSpec as P

EPS = 1e-6


def rms_norm(vals):
    wide = vals.astype(jnp.float32)
    return wide * lax.rsqrt(jnp.mean(wide * wide, axis=-1, keepdims=True) + EPS)


def attention_layer(tokens, w_query, w_key, w_value, w_out):
    seq_count = tokens.shape[0]
    seq_len = tokens.shape[1]
    head_dim = w_query.shape[2]
    normed = rms_norm(tokens).astype(jnp.bfloat16)
    query = jnp.einsum('bsd,dhk->bshk', normed, w_query, preferred_element_type=jnp.float32).astype(jnp.bfloat16)
    keys = jnp.einsum('bsd,dhk->bshk', normed, w_key, preferred_element_type=jnp.float32).astype(jnp.bfloat16)
    values = jnp.einsum('bsd,dhk->bshk', normed, w_value, preferred_element_type=jnp.float32).astype(jnp.bfloat16)
    scores = jnp.einsum('bqhk,bshk->bhqs', query, keys, preferred_element_type=jnp.float32) * head_dim ** -0.5
    causal = lax.broadcasted_iota(jnp.int32, (seq_len, seq_len), 0) >= lax.broadcasted_iota(jnp.int32, (seq_len, seq_len), 1)
    attn_weights = jax.nn.softmax(jnp.where(causal, scores, -jnp.inf), axis=-1).astype(jnp.bfloat16)
    context = jnp.einsum('bhqs,bshk->bqhk', attn_weights, values, preferred_element_type=jnp.float32).astype(jnp.bfloat16)
    attn_out = jnp.einsum('crd,de->cre', context.reshape(seq_count, seq_len, -1), w_out, preferred_element_type=jnp.float32)
    return (tokens.astype(jnp.float32) + attn_out).astype(jnp.bfloat16)


def router_gates(hidden, w_router, expert_ids):
    normed = rms_norm(hidden)
    logits = jnp.einsum('bsd,de->bse', normed, w_router, precision=lax.Precision.HIGHEST, preferred_element_type=jnp.float32)
    chosen = jnp.take_along_axis(logits, expert_ids, axis=-1)
    return normed.astype(jnp.bfloat16), jax.nn.softmax(chosen, axis=-1)


def dispatch_tables(ids_flat, experts, cap_rows):
    member = jnp.sum((ids_flat[:, :, None] == jnp.arange(experts, dtype=jnp.int32)).astype(jnp.int32), axis=1)
    before = jnp.cumsum(member, axis=0) - member
    slot = jnp.take_along_axis(before, ids_flat, axis=1)
    onehot = (member[:, :, None] > 0) & (before[:, :, None] == jnp.arange(cap_rows, dtype=jnp.int32))
    return onehot.astype(jnp.bfloat16), ids_flat * cap_rows + slot


def expert_ffn(rows, w_one, w_three, w_two):
    first = jnp.einsum('end,edf->enf', rows, w_one, preferred_element_type=jnp.float32)
    third = jnp.einsum('end,edf->enf', rows, w_three, preferred_element_type=jnp.float32)
    activated = (jax.nn.silu(first) * third).astype(jnp.bfloat16)
    return jnp.einsum('enf,efd->end', activated, w_two, preferred_element_type=jnp.float32).astype(jnp.bfloat16)


def combine_rows(hidden_flat, back_rows, flat_slot, gates_flat):
    table = back_rows.reshape(-1, back_rows.shape[-1])
    picked = jnp.take(table, flat_slot, axis=0)
    mixed = jnp.sum(gates_flat[:, :, None] * picked.astype(jnp.float32), axis=1)
    return (hidden_flat.astype(jnp.float32) + mixed).astype(jnp.bfloat16)


def solution(mesh):
    tok_spec = P(('dp', 'ep'))
    row_spec = P('ep')

    def local_layer(tokens, w_query, w_key, w_value, w_out, w_router, w_one, w_three, w_two, expert_ids):
        full_query = lax.all_gather(w_query, 'ep', axis=0, tiled=True)
        full_key = lax.all_gather(w_key, 'ep', axis=0, tiled=True)
        full_value = lax.all_gather(w_value, 'ep', axis=0, tiled=True)
        full_out = lax.all_gather(w_out, 'ep', axis=0, tiled=True)
        hidden = attention_layer(tokens, full_query, full_key, full_value, full_out)
        normed, gates = router_gates(hidden, w_router, expert_ids)
        seq_count, seq_len, model_dim = tokens.shape
        choices = expert_ids.shape[2]
        experts = w_router.shape[1]
        tok_count = seq_count * seq_len
        cap_rows = 2 * tok_count * choices // experts
        onehot, flat_slot = dispatch_tables(expert_ids.reshape(tok_count, choices), experts, cap_rows)
        send_rows = jnp.einsum('tec,td->ecd', onehot, normed.reshape(tok_count, model_dim), preferred_element_type=jnp.float32).astype(jnp.bfloat16)
        recv_rows = lax.all_to_all(send_rows, 'ep', 0, 1, tiled=True)
        done_rows = expert_ffn(recv_rows, w_one, w_three, w_two)
        back_rows = lax.all_to_all(done_rows, 'ep', 1, 0, tiled=True)
        layer_out = combine_rows(hidden.reshape(tok_count, model_dim), back_rows, flat_slot, gates.reshape(tok_count, choices))
        return layer_out.reshape(seq_count, seq_len, model_dim)

    return jax.shard_map(local_layer, mesh=mesh, in_specs=(tok_spec, row_spec, row_spec, row_spec, row_spec, P(), row_spec, row_spec, row_spec, tok_spec), out_specs=tok_spec, check_vma=False)
```

profile of v0, /device:TPU:21, one launch (start us, length us, event | category | flops | bytes accessed | tf_op | source)
XLA Modules:
  0.0 1083.0 jit_solution(3708637360433247243)
XLA Ops:
  6.6 0.7 all-gather.9.cloned.1.call-update
  7.4 0.7 all-gather.7.cloned.1.call-update
  9.6 0.8 iota_compare_fusion.1
  10.3 0.8 convert_reduce_fusion
  11.5 1.2 reduce-window.6
  13.0 39.7 %all-gather.9.cloned.1.call-done = bf16[1024,16,64]{2,1,0:T(8,128)(2,1)} async-done(((bf16[64,16,64]{2,1,0:T(8,128)(2,1)}), bf16[1024,16,64]{2,1,0:T(8,128)(2,1)}) %all-gather.9.cloned.1.call-update) | async-done | bytes 2097168 | tf_op jit(solution)/shard_map/all_gather | solution.py:65
  52.7 5.5 copy.64
  58.2 33.0 %all-gather.7.cloned.1.call-done = bf16[1024,16,64]{2,1,0:T(8,128)(2,1)} async-done(((bf16[64,16,64]{2,1,0:T(8,128)(2,1)}), bf16[1024,16,64]{2,1,0:T(8,128)(2,1)}) %all-gather.7.cloned.1.call-update) | async-done | bytes 2097168 | tf_op jit(solution)/shard_map/all_gather | solution.py:64
  91.2 5.5 copy.63
  96.7 33.1 %all-gather.5.cloned.1.call-done = bf16[1024,16,64]{2,1,0:T(8,128)(2,1)} async-done(((bf16[64,16,64]{2,1,0:T(8,128)(2,1)}), bf16[1024,16,64]{2,1,0:T(8,128)(2,1)}) %all-gather.5.cloned.1.call-update) | async-done | bytes 2097168 | tf_op jit(solution)/shard_map/all_gather | solution.py:66
  129.7 5.5 copy.62
  135.3 4.4 fusion.53
  139.7 2.7 fusion.55
  142.4 3.4 fusion.57
  145.8 10.7 fusion.59
  156.5 9.0 fusion.28
  165.7 3.3 fusion.24
  169.0 13.1 %fusion.5 = bf16[32,256,1024]{2,1,0:T(8,128)(2,1)} fusion(s32[512,32]{0,1:T(8,128)S(1)} %fusion.46, pred[512,32]{0,1:T(8,128)(4,1)S(1)} %broadcast_compare_fusion, bf16[1,512,1024]{2,1,0:T(8,128)(2,1)S(1)} %get-tuple-element.10, f32[512]{0:T(512)S(1)} %add_rsqrt_fusion), kind=kOutput, calls=%fused_computation.14 | convolution fusion | flops 8608284672 | bytes 17909760 | tf_op jit(solution)/shard_map/tec,td->ecd/dot_general | solution.py:76
  182.1 370.1 %all_to_all.33 = bf16[32,256,1024]{2,1,0:T(8,128)(2,1)S(1)} all-to-all(bf16[32,256,1024]{2,1,0:T(8,128)(2,1)} %fusion.5), channel_id=1, replica_groups=mesh['dp'=4,'ep'=16] {'ep'}, dimensions={0} | all-to-all | bytes 33554432 | tf_op jit(solution)/shard_map/all_to_all | solution.py:77
  552.2 6.7 copy.74
  558.9 18.5 %fusion.68 = f32[2,4096,512]{2,1,0:T(8,128)} fusion(bf16[2,4096,1024]{2,1,0:T(8,128)(2,1)} %bitcast.92, bf16[2,1024,512]{2,1,0:T(8,128)(2,1)} %param.16), kind=kOutput, calls=%fused_computation.85 | convolution fusion | flops 8589934592 | bytes 35651584 | tf_op jit(solution)/shard_map/end,edf->enf/dot_general | solution.py:46
  577.3 27.0 %convolution_convert_fusion = bf16[2,4096,1024]{2,1,0:T(8,128)(2,1)} fusion(bf16[2,512,1024]{2,1,0:T(8,128)(2,1)S(1)} %copy-done, f32[2,4096,512]{2,1,0:T(8,128)} %fusion.68, bf16[2,4096,1024]{2,1,0:T(8,128)(2,1)} %bitcast.93, bf16[2,1024,512]{2,1,0:T(8,128)(2,1)} %param.17), kind=kOutput, calls=%fused_computation.13 | convolution fusion | flops 17213423616 | bytes 54525952 | tf_op jit(solution)/shard_map/enf,efd->end/dot_general | solution.py:49
  604.3 31.0 %copy.75 = bf16[2,4096,1024]{2,0,1:T(2,128)(2,1)} copy(bf16[2,4096,1024]{2,1,0:T(8,128)(2,1)} %convolution_convert_fusion) | data formatting | bytes 33554432 | tf_op jit(solution)/shard_map/convert_element_type | solution.py:49
  635.3 5.6 all-to-all-start.1
  641.2 33.0 %gather_fusion.2 = s32[4096]{0:T(1024)S(1)} fusion(s32[512,32]{0,1:T(8,128)S(1)} %fusion.46, s32[4096]{0:T(1024)S(1)} %reshape.270), kind=kCustom, calls=%fused_computation.2 | custom fusion | bytes 65536 | tf_op jit(solution)/shard_map/jit(take_along_axis)/gather | solution.py:40
  675.6 2.2 fusion.19
  677.9 33.0 %gather_fusion.1 = f32[4096]{0:T(1024)S(1)} fusion(f32[512,32]{0,1:T(8,128)S(1)} %fusion.19, s32[4096]{0:T(1024)S(1)} %reshape.264), kind=kCustom, calls=%fused_computation.1 | custom fusion | bytes 65536 | tf_op jit(solution)/shard_map/jit(take_along_axis)/gather | solution.py:33
  711.4 309.1 %all-to-all-done.1 = bf16[2,4096,1024]{2,0,1:T(2,128)(2,1)} async-done(((bf16[2,4096,1024]{2,0,1:T(2,128)(2,1)}), bf16[2,4096,1024]{2,0,1:T(2,128)(2,1)}, u32[]{:S(2)}, u32[]{:S(2)}) %all-to-all-start.1) | async-done | bytes 16777248 | tf_op jit(solution)/shard_map/all_to_all | solution.py:79
  1020.5 16.4 %copy.76 = bf16[2,16,256,1024]{3,2,0,1:T(8,128)(2,1)} copy(bf16[2,16,256,1024]{3,0,2,1:T(2,128)(2,1)} %bitcast.23) | data formatting | bytes 33554432 | tf_op jit(solution)/shard_map/all_to_all | solution.py:79
  1036.9 28.8 %gather_fusion = bf16[4096,1024]{1,0:T(8,128)(2,1)} fusion(bf16[8192,1024]{1,0:T(8,128)(2,1)} %bitcast.90, s32[4096]{0:T(1024)S(1)} %broadcast_clamp_fusion), kind=kCustom, calls=%fused_computation | custom fusion | bytes 16793600 | tf_op jit(solution)/shard_map/jit(_take)/gather | solution.py:54
  1065.7 9.2 multiply_reduce_fusion
  1074.9 1.3 fusion.25
  (63 shorter events, 4.4 us)
Async XLA Ops:
  6.5 570.8 %copy-start = (bf16[2,512,1024]{2,1,0:T(8,128)(2,1)S(1)}, bf16[2,512,1024]{2,1,0:T(8,128)(2,1)}, u32[]{:S(2)}) copy-start(bf16[2,512,1024]{2,1,0:T(8,128)(2,1)} %param.18) | copy-start | bytes 6291460
  6.6 4.6 copy-start.6
  6.6 46.1 %all-gather.9.cloned.1.call-start = ((), (), s32[]{:S(2)}) async-start(), calls=%async_computation.4 | async-start | bytes 4456448 | tf_op jit(solution)/shard_map/all_gather | solution.py:65
  7.3 83.9 %all-gather.7.cloned.1.call-start = ((), (), s32[]{:S(2)}) async-start(), calls=%async_computation.3 | async-start | bytes 4456448 | tf_op jit(solution)/shard_map/all_gather | solution.py:64
  8.1 121.6 %all-gather.5.cloned.1.call-start = ((), (), s32[]{:S(2)}) async-start(), calls=%async_computation.2 | async-start | bytes 4456448 | tf_op jit(solution)/shard_map/all_gather | solution.py:66
  8.9 156.8 %all-gather.11.cloned.1.call-start = ((), (), s32[]{:S(2)}) async-start(), calls=%async_computation.5 | async-start | bytes 2228224 | tf_op jit(solution)/shard_map/all_gather | solution.py:67
  11.4 128.2 %copy-start.12 = (f32[512]{0:T(512)}, f32[512]{0:T(512)S(1)}, u32[]{:S(2)}) copy-start(f32[512]{0:T(512)S(1)} %add_rsqrt_fusion.1) | copy-start | bytes 6148
  135.2 4.4 copy-start.4
  139.7 2.7 copy-start.5
  142.3 3.4 copy-start.8
  169.0 13.1 %copy-start.2 = (bf16[1,512,1024]{2,1,0:T(8,128)(2,1)}, bf16[1,512,1024]{2,1,0:T(8,128)(2,1)S(1)}, u32[]{:S(2)}) copy-start(bf16[1,512,1024]{2,1,0:T(8,128)(2,1)S(1)} %get-tuple-element.10) | copy-start | bytes 3145732
  169.0 13.1 %copy-start.10 = (f32[512]{0:T(512)}, f32[512]{0:T(512)S(1)}, u32[]{:S(2)}) copy-start(f32[512]{0:T(512)S(1)} %add_rsqrt_fusion) | copy-start | bytes 6148
  635.3 5.6 copy-start.7
  635.3 385.2 %all-to-all-start.1 = ((bf16[2,4096,1024]{2,0,1:T(2,128)(2,1)}), bf16[2,4096,1024]{2,0,1:T(2,128)(2,1)}, u32[]{:S(2)}, u32[]{:S(2)}) async-start(bf16[2,4096,1024]{2,0,1:T(2,128)(2,1)} %copy.75), calls=%async_computation.1 | async-start | bytes 33554432 | tf_op jit(solution)/shard_map/all_to_all | solution.py:79
  674.2 1.4 copy-start.3
  674.3 1.4 copy-start.9
  674.3 1.4 copy-start.11
  1065.7 10.5 copy-start.1
Sparse Core Ops, SparseCore 0:
  9.0 43.6 all-gather.8
  54.3 36.8 all-gather.6
  92.8 36.8 all-gather.4
  131.2 34.4 all-gather.10
where the time goes:
time: 1100 us; the launch traced here: 1080 us
  waiting for transfers between devices  418 us (38%)
  blocking collectives  370 us (34%)
  local copies, waits for them, and re-layouts  168 us (15%)
  matrix products  94.2 us (9%)
  other arithmetic  13.8 us (1%)
  between operations  13.6 us (1%)
    all_to_all x1, blocking collectives, local_layer(): recv_rows = lax.all_to_all(send_rows, 'ep', 0, 1, tiled=True)  370 us
    all_to_all x1, waiting for transfers between devices, local_layer(): back_rows = lax.all_to_all(done_rows, 'ep', 1, 0, tiled=True)  309 us
    all_gather x1, waiting for transfers between devices, local_layer(): full_key = lax.all_gather(w_key, 'ep', axis=0, tiled=True)  39.7 us
    gather x7, local copies, waits for them, and re-layouts, dispatch_tables(): slot = jnp.take_along_axis(before, ids_flat, axis=1)  33.8 us
    gather x5, local copies, waits for them, and re-layouts, router_gates(): chosen = jnp.take_along_axis(logits, expert_ids, axis=-1)  33.6 us
    all_gather x1, waiting for transfers between devices, local_layer(): full_value = lax.all_gather(w_value, 'ep', axis=0, tiled=True)  33.1 us
    all_gather x1, waiting for transfers between devices, local_layer(): full_query = lax.all_gather(w_query, 'ep', axis=0, tiled=True)  33 us
    convert_element_type x1, local copies, waits for them, and re-layouts, expert_ffn(): jnp.einsum('enf,efd->end', activated, w_two, preferred_element_type=jnp.f...  31 us
  transfers between devices with their start and end apart: 5, of which 5 were waited for; matrix products, arithmetic and copies ran while one was open for 11% of the time, Pallas kernels for 0%

commit v1 on v0

v1 whole, which is shorter than its diff:
```python
import functools

import jax
import jax.numpy as jnp
from jax import lax
from jax.experimental import pallas as pl
from jax.experimental.pallas import tpu as pltpu
from jax.sharding import PartitionSpec as P

EPS = 1e-6
MESH = pl.DeviceIdType.MESH


def rms_norm(vals):
    wide = vals.astype(jnp.float32)
    return wide * lax.rsqrt(jnp.mean(wide * wide, axis=-1, keepdims=True) + EPS)


def attention_layer(tokens, w_query, w_key, w_value, w_out):
    seq_count = tokens.shape[0]
    seq_len = tokens.shape[1]
    head_dim = w_query.shape[2]
    normed = rms_norm(tokens).astype(jnp.bfloat16)
    query = jnp.einsum('bsd,dhk->bshk', normed, w_query, preferred_element_type=jnp.float32).astype(jnp.bfloat16)
    keys = jnp.einsum('bsd,dhk->bshk', normed, w_key, preferred_element_type=jnp.float32).astype(jnp.bfloat16)
    values = jnp.einsum('bsd,dhk->bshk', normed, w_value, preferred_element_type=jnp.float32).astype(jnp.bfloat16)
    scores = jnp.einsum('bqhk,bshk->bhqs', query, keys, preferred_element_type=jnp.float32) * head_dim ** -0.5
    causal = lax.broadcasted_iota(jnp.int32, (seq_len, seq_len), 0) >= lax.broadcasted_iota(jnp.int32, (seq_len, seq_len), 1)
    attn_weights = jax.nn.softmax(jnp.where(causal, scores, -jnp.inf), axis=-1).astype(jnp.bfloat16)
    context = jnp.einsum('bhqs,bshk->bqhk', attn_weights, values, preferred_element_type=jnp.float32).astype(jnp.bfloat16)
    attn_out = jnp.einsum('crd,de->cre', context.reshape(seq_count, seq_len, -1), w_out, preferred_element_type=jnp.float32)
    return (tokens.astype(jnp.float32) + attn_out).astype(jnp.bfloat16)


def router_gates(hidden, w_router, expert_ids):
    normed = rms_norm(hidden)
    logits = jnp.dot(normed, w_router, precision=lax.Precision.HIGHEST, preferred_element_type=jnp.float32)
    chosen = jnp.take_along_axis(logits, expert_ids, axis=-1)
    gates = jax.nn.softmax(chosen, axis=-1)
    experts = w_router.shape[1]
    match = expert_ids[:, :, None] == jnp.arange(experts, dtype=jnp.int32)
    dense = jnp.sum(jnp.where(match, gates[:, :, None], 0.0), axis=1)
    return normed.astype(jnp.bfloat16), dense.T


def moe_kernel(n, hops, u_hbm, g_ref, h_ref, w1_hbm, w3_hbm, w2_hbm, y_ref,
               ubuf, gbuf, part, acc, w1, w3, w2,
               u_send, u_recv, a_send, a_recv, g_send, g_recv, w_send, w_recv, w_loc, u_loc, *, pieces_u, pieces_a):
    me = lax.axis_index('ep')
    pos, core = lax.div(me, 2), lax.rem(me, 2)
    tok, half = ubuf.shape[1], ubuf.shape[1] // 2
    own = w1_hbm.shape[0]
    total = w1.shape[0]
    ru, ra = half // pieces_u, half // pieces_a

    def peer(z):
        return {'ep': lax.rem(z + 2 * n, n) * 2 + core}

    sibling = {'ep': pos * 2 + (1 - core)}

    barrier = pltpu.get_barrier_semaphore()
    for k in range(1, n):
        pl.semaphore_signal(barrier, inc=1, device_id=peer(pos + k), device_id_type=MESH)
    pl.semaphore_signal(barrier, inc=1, device_id=sibling, device_id_type=MESH)

    own_copy = pltpu.make_async_copy(u_hbm, ubuf.at[0], u_loc.at[0])
    own_copy.start()
    mine = pl.ds(core * own, own)
    loads = []
    for i, (src, dst) in enumerate(((w1_hbm, w1), (w3_hbm, w3), (w2_hbm, w2))):
        loads.append(pltpu.make_async_copy(src, dst.at[mine], w_loc.at[i]))
        loads[-1].start()
    pl.semaphore_wait(barrier, n)

    def u_copy(d, s, p):
        rows = pl.ds(d * half + p * ru, ru)
        return pltpu.make_async_remote_copy(
            src_ref=ubuf.at[s, rows], dst_ref=ubuf.at[s + 1, rows],
            send_sem=u_send.at[d, s, p], recv_sem=u_recv.at[d, s, p],
            device_id=peer(pos + (1 if d == 0 else n - 1)), device_id_type=MESH)

    def a_copy(d, s, p):
        rows = pl.ds(d * half + p * ra, ra)
        return pltpu.make_async_remote_copy(
            src_ref=part.at[s, rows], dst_ref=acc.at[s - 1, rows],
            send_sem=a_send.at[d, s - 1, p], recv_sem=a_recv.at[d, s - 1, p],
            device_id=peer(pos + (n - 1 if d == 0 else 1)), device_id_type=MESH)

    def g_copy(d, s):
        cols = pl.ds(d * half, half)
        target = pos + (s if d == 0 else n - s)
        return pltpu.make_async_remote_copy(
            src_ref=g_ref.at[lax.rem(target, g_ref.shape[0]), :, cols], dst_ref=gbuf.at[s - 1, :, cols],
            send_sem=g_send.at[d, s - 1], recv_sem=g_recv.at[d, s - 1],
            device_id=peer(target), device_id_type=MESH)

    def w_copy(i, src, dst):
        return pltpu.make_async_remote_copy(
            src_ref=src, dst_ref=dst.at[mine], send_sem=w_send.at[i], recv_sem=w_recv.at[i],
            device_id=sibling, device_id_type=MESH)

    own_copy.wait()
    for p in range(pieces_u):
        for d in range(2):
            u_copy(d, 0, p).start()
    w_copies = [w_copy(i, s, t) for i, (s, t) in enumerate(((w1_hbm, w1), (w3_hbm, w3), (w2_hbm, w2)))]
    for c in w_copies:
        c.start()
    for s in range(1, hops + 1):
        for d in range(2):
            g_copy(d, s).start()

    def experts(s, gates_t, first, count):
        gates = gates_t.T

        def one(e, _):
            lane = lax.broadcasted_iota(jnp.int32, gates.shape, 1)
            g = jnp.sum(jnp.where(lane == e, gates, 0.0), axis=1, keepdims=True)
            x = ubuf[s]
            f1 = jnp.dot(x, w1[e], preferred_element_type=jnp.float32)
            f3 = jnp.dot(x, w3[e], preferred_element_type=jnp.float32)
            a = (f1 * jax.nn.sigmoid(f1) * f3).astype(jnp.bfloat16)
            width = w2.shape[2]
            for j in range(0, width, 512):
                o = jnp.dot(a, w2[e, :, j:j + 512], preferred_element_type=jnp.float32).astype(jnp.bfloat16).astype(jnp.float32)
                part[s, :, j:j + 512] += jnp.where(g != 0.0, g * o, 0.0)
            return 0

        lax.fori_loop(first, first + count, one, 0)

    for c in loads:
        c.wait()
    for c in w_copies:
        c.wait()
    for s in range(1, hops + 1):
        for d in range(2):
            g_copy(d, s).wait()

    def visit(s, _):
        part[s] = jnp.zeros(part.shape[1:], jnp.float32)

        @pl.when(s == 0)
        def _():
            experts(s, g_ref[lax.rem(pos, g_ref.shape[0])], 0, total)

        @pl.when(s > 0)
        def _():
            for p in range(pieces_u):
                for d in range(2):
                    u_copy(d, s - 1, p).wait_recv()

                    @pl.when(s < hops)
                    def _():
                        u_copy(d, s, p).start()
            experts(s, gbuf[s - 1], 0, total)

        return 0

    lax.fori_loop(0, hops + 1, visit, 0)

    def back(i, _):
        s = hops - i
        for p in range(pieces_a):
            for d in range(2):
                rows = pl.ds(d * half + p * ra, ra)

                @pl.when(i > 0)
                def _():
                    a_copy(d, s + 1, p).wait_recv()
                    part[s, rows] += acc[s, rows]

                @pl.when(s > 0)
                def _():
                    a_copy(d, s, p).start()

                @pl.when(s == 0)
                def _():
                    y_ref[rows] = (h_ref[rows].astype(jnp.float32) + part[s, rows]).astype(y_ref.dtype)
        return 0

    lax.fori_loop(0, hops + 1, back, 0)

    def drain(s, _):
        for d in range(2):
            for p in range(pieces_u):
                u_copy(d, s, p).wait_send()
            for p in range(pieces_a):
                a_copy(d, s + 1, p).wait_send()
        return 0

    lax.fori_loop(0, hops, drain, 0)


def moe(u, gates, hidden, w_one, w_three, w_two, n, hops):
    tok, dim = u.shape
    own, _, ff = w_one.shape
    total = 2 * own
    pieces_u, pieces_a = 2, 4
    dma = pltpu.SemaphoreType.DMA
    any_spec = pl.BlockSpec(memory_space=pl.ANY)
    vmem = pl.BlockSpec(memory_space=pltpu.VMEM)
    return pl.pallas_call(
        functools.partial(moe_kernel, n, hops, pieces_u=pieces_u, pieces_a=pieces_a),
        out_shape=jax.ShapeDtypeStruct((tok, dim), jnp.bfloat16),
        in_specs=[any_spec, vmem, vmem, any_spec, any_spec, any_spec],
        out_specs=vmem,
        scratch_shapes=[
            pltpu.VMEM((hops + 1, tok, dim), jnp.bfloat16),
            pltpu.VMEM((hops, gates.shape[1], tok), jnp.float32),
            pltpu.VMEM((hops + 1, tok, dim), jnp.float32),
            pltpu.VMEM((hops, tok, dim), jnp.float32),
            pltpu.VMEM((total, dim, ff), jnp.bfloat16),
            pltpu.VMEM((total, dim, ff), jnp.bfloat16),
            pltpu.VMEM((total, ff, dim), jnp.bfloat16),
            dma((2, hops, pieces_u)), dma((2, hops, pieces_u)),
            dma((2, hops, pieces_a)), dma((2, hops, pieces_a)),
            dma((2, hops)), dma((2, hops)),
            dma((3,)), dma((3,)), dma((3,)), dma((1,)),
        ],
        compiler_params=pltpu.CompilerParams(collective_id=1, has_side_effects=True, vmem_limit_bytes=66_000_000),
        name='moe_ring',
    )(u, gates, hidden, w_one, w_three, w_two)


def solution(mesh):
    tok_spec = P(('dp', 'ep'))
    row_spec = P('ep')
    n = mesh.shape['ep'] // 2

    def local_layer(tokens, w_query, w_key, w_value, w_out, w_router, w_one, w_three, w_two, expert_ids):
        full_query = lax.all_gather(w_query, 'ep', axis=0, tiled=True)
        full_key = lax.all_gather(w_key, 'ep', axis=0, tiled=True)
        full_value = lax.all_gather(w_value, 'ep', axis=0, tiled=True)
        full_out = lax.all_gather(w_out, 'ep', axis=0, tiled=True)
        hidden = attention_layer(tokens, full_query, full_key, full_value, full_out)
        tok, dim = tokens.shape[0] * tokens.shape[1], tokens.shape[2]
        hidden = hidden.reshape(tok, dim)
        u, gates = router_gates(hidden, w_router, expert_ids.reshape(tok, -1))
        per = gates.shape[0] // n
        gates = jnp.pad(gates.reshape(n, per, tok), ((0, 0), (0, 8 - per), (0, 0)))
        out = moe(u, gates, hidden, w_one, w_three, w_two, n, n - 1)
        return out.reshape(tokens.shape)

    return jax.shard_map(local_layer, mesh=mesh, in_specs=(tok_spec, row_spec, row_spec, row_spec, row_spec, P(), row_spec, row_spec, row_spec, tok_spec), out_specs=tok_spec, check_vma=False)
```

time: 1100 us -> 483 us (0.44); the launches traced: 1080 us -> 481 us
  blocking collectives: 370 us -> 0 us
  waiting for transfers between devices: 418 us -> 113 us
  Pallas kernels: 0 us -> 266 us
  local copies, waits for them, and re-layouts: 168 us -> 52.2 us
  matrix products: 94.2 us -> 33.2 us
    all_to_all x1 -> x0, blocking collectives: 370 us -> none  [local_layer(): recv_rows = lax.all_to_all(send_rows, 'ep', 0, 1, tiled=True)]
    all_to_all x1 -> x0, waiting for transfers between devices: 309 us -> none  [local_layer(): back_rows = lax.all_to_all(done_rows, 'ep', 1, 0, tiled=True)]
    pallas_call x0 -> x1, Pallas kernels: none -> 266 us  [moe(): pl.pallas_call(functools.partial(moe_kernel, n, hops, pieces_u=pieces_u,...]
    gather x8 -> x0, local copies, waits for them, and re-layouts: 62.6 us -> none  [the longest x7 33.8 us: dispatch_tables(): slot = jnp.take_along_axis(before, ids_flat, axis=1)]
    dot_general x4 -> x1, matrix products: 60.7 us -> 2.22 us  [router_gates(): jnp.dot(normed, w_router, precision=lax.Precision.HIGHEST, preferred_elem...]
    convert_element_type x1 -> x0, local copies, waits for them, and re-layouts: 31 us -> none  [expert_ffn(): jnp.einsum('enf,efd->end', activated, w_two, preferred_element_type=jnp.f...]
    all_to_all x2 -> x0, local copies, waits for them, and re-layouts: 23.1 us -> none  [the longest x1 16.4 us: local_layer(): back_rows = lax.all_to_all(done_rows, 'ep', 1, 0, tiled=True)]
  transfers between devices with their start and end apart: 5 -> 4, of which waited for: 5 -> 4; matrix products, arithmetic and copies ran while one was open for 11% -> 10% of each run, Pallas kernels for 0% -> 0%
where the time goes in v1:
time: 483 us; the launch traced here: 481 us
  Pallas kernels  266 us (55%)
  waiting for transfers between devices  113 us (23%)
  local copies, waits for them, and re-layouts  52.2 us (11%)
  matrix products  33.2 us (7%)
  between operations  13.3 us (3%)
    pallas_call x1, Pallas kernels, moe(): pl.pallas_call(functools.partial(moe_kernel, n, hops, pieces_u=pieces_u,...  266 us
    all_gather x1, waiting for transfers between devices, local_layer(): full_query = lax.all_gather(w_query, 'ep', axis=0, tiled=True)  40.5 us
    all_gather x1, waiting for transfers between devices, local_layer(): full_key = lax.all_gather(w_key, 'ep', axis=0, tiled=True)  34 us
    gather x5, local copies, waits for them, and re-layouts, router_gates(): chosen = jnp.take_along_axis(logits, expert_ids, axis=-1)  33.7 us
    all_gather x1, waiting for transfers between devices, local_layer(): full_value = lax.all_gather(w_value, 'ep', axis=0, tiled=True)  33 us
    sub x1, matrix products, attention_layer(): jax.nn.softmax(jnp.where(causal, scores, -jnp.inf), axis=-1)  10.7 us
  transfers between devices with their start and end apart: 4, of which 4 were waited for; matrix products, arithmetic and copies ran while one was open for 10% of the time, Pallas kernels for 0%

profile of v1, /device:TPU:21, one launch (start us, length us, event | category | flops | bytes accessed | tf_op | source)
XLA Modules:
  0.0 481.2 jit_solution(7551439514266482535)
XLA Ops:
  6.6 0.7 all-gather.7.cloned.1.call-update
  7.3 0.1 all-gather.9.cloned.1.call-start
  7.4 0.7 all-gather.9.cloned.1.call-update
  8.1 0.1 all-gather.5.cloned.1.call-start
  8.2 0.7 all-gather.5.cloned.1.call-update
  8.9 0.1 all-gather.11.cloned.1.call-start
  9.0 0.6 all-gather.11.cloned.1.call-update
  9.6 0.8 iota_compare_fusion
  10.3 1.5 fusion.9
  11.9 0.1 copy.35
  12.0 0.2 reshape.166
  12.2 40.5 %all-gather.7.cloned.1.call-done = bf16[1024,16,64]{2,1,0:T(8,128)(2,1)} async-done(((bf16[64,16,64]{2,1,0:T(8,128)(2,1)}), bf16[1024,16,64]{2,1,0:T(8,128)(2,1)}) %all-gather.7.cloned.1.call-update) | async-done | bytes 2097168 | tf_op jit(solution)/shard_map/all_gather | solution.py:231
  52.7 4.5 copy.32
  57.2 34.0 %all-gather.9.cloned.1.call-done = bf16[1024,16,64]{2,1,0:T(8,128)(2,1)} async-done(((bf16[64,16,64]{2,1,0:T(8,128)(2,1)}), bf16[1024,16,64]{2,1,0:T(8,128)(2,1)}) %all-gather.9.cloned.1.call-update) | async-done | bytes 2097168 | tf_op jit(solution)/shard_map/all_gather | solution.py:232
  91.2 5.5 %copy.33 = bf16[1024,16,64]{0,2,1:T(8,128)(2,1)} copy(bf16[1024,16,64]{2,1,0:T(8,128)(2,1)} %all-gather.9.cloned.1.call-done) | data formatting | bytes 4194304 | tf_op jit(solution)/shard_map/all_gather | solution.py:232
  96.7 33.0 %all-gather.5.cloned.1.call-done = bf16[1024,16,64]{2,1,0:T(8,128)(2,1)} async-done(((bf16[64,16,64]{2,1,0:T(8,128)(2,1)}), bf16[1024,16,64]{2,1,0:T(8,128)(2,1)}) %all-gather.5.cloned.1.call-update) | async-done | bytes 2097168 | tf_op jit(solution)/shard_map/all_gather | solution.py:233
  129.7 5.5 %copy.31 = bf16[1024,16,64]{0,2,1:T(8,128)(2,1)} copy(bf16[1024,16,64]{2,1,0:T(8,128)(2,1)} %all-gather.5.cloned.1.call-done) | data formatting | bytes 4194304 | tf_op jit(solution)/shard_map/all_gather | solution.py:233
  135.3 2.7 fusion.40
  137.9 2.7 fusion.38
  140.6 2.7 fusion.42
  143.3 10.7 %fusion.44 = (f32[16,512]{1,0:T(8,128)S(1)}, f32[16,512,512]{1,2,0:T(8,128)}) fusion(pred[512,512]{0,1:T(8,128)(4,1)S(1)} %copy-done.6, f32[512,16,64]{0,2,1:T(8,128)} %bitcast.50, f32[512,16,64]{0,2,1:T(8,128)} %bitcast.48), kind=kOutput, calls=%fused_computation.52 | convolution fusion | flops 554697216 | bytes 21266432 | tf_op jit(solution)/shard_map/sub | solution.py:29
  154.0 9.0 %fusion.14 = bf16[16,64,512]{2,1,0:T(8,128)(2,1)} fusion(f32[16,512,512]{1,2,0:T(8,128)} %get-tuple-element.6, f32[16,512]{1,0:T(8,128)S(1)} %get-tuple-element.5, f32[512,16,64]{0,2,1:T(8,128)} %bitcast.49), kind=kOutput, calls=%fused_computation.22 | convolution fusion | flops 546308096 | bytes 19955712 | tf_op jit(solution)/shard_map/bhqs,bshk->bqhk/dot_general | solution.py:30
  163.0 2.7 all-gather.11.cloned.1.call-done
  165.7 3.3 fusion.8
  169.0 1.3 fusion.7.u_hbm
  170.3 2.2 fusion.6
  172.5 33.2 %gather_fusion = f32[4096]{0:T(1024)S(1)} fusion(f32[512,32]{0,1:T(8,128)S(1)} %fusion.6, s32[4096]{0:T(1024)S(1)} %reshape.166), kind=kCustom, calls=%fused_computation | custom fusion | bytes 65536 | tf_op jit(solution)/shard_map/jit(take_along_axis)/gather | solution.py:38
  205.8 0.2 reshape.169
  205.9 0.1 copy.36
  206.2 0.7 pad.4.g_ref
  206.9 265.5 %moe_ring.1 = bf16[512,1024]{1,0:T(8,128)(2,1)} custom-call(bf16[512,1024]{1,0:T(8,128)(2,1)} %fusion.7.u_hbm, f32[8,8,512]{2,1,0:T(8,128)} %pad.4.g_ref, bf16[512,1024]{1,0:T(8,128)(2,1)} %copy-done.1, bf16[2,1024,512]{2,1,0:T(8,128)(2,1)} %w1_hbm.1, bf16[2,1024,512]{2,1,0:T(8,128)(2,1)} %w3_hbm.1, bf16[2,512,1024]{2,1,0:T(8,128)(2,1)} %w2_hbm.1), custom_call_target="tpu_custom_call" | custom-call | tf_op jit(solution)/shard_map/moe_ring/pallas_call | solution.py:202
  472.4 2.3 copy.39
  (23 shorter events, 0.2 us)
Async XLA Ops:
  6.5 163.8 %copy-start = (f32[1024,32]{0,1:T(8,128)S(1)}, f32[1024,32]{0,1:T(8,128)}, u32[]{:S(2)}) copy-start(f32[1024,32]{0,1:T(8,128)} %param.15) | copy-start | bytes 393220
  6.6 5.3 %copy-start.5 = (s32[1,512,8]{1,2,0:T(8,128)S(1)}, s32[1,512,8]{1,2,0:T(8,128)}, u32[]{:S(2)}) copy-start(s32[1,512,8]{1,2,0:T(8,128)} %param.19) | copy-start | bytes 49156
  6.6 46.1 %all-gather.7.cloned.1.call-start = ((), (), s32[]{:S(2)}) async-start(), calls=%async_computation.1 | async-start | bytes 4456448 | tf_op jit(solution)/shard_map/all_gather | solution.py:231
  7.3 83.9 %all-gather.9.cloned.1.call-start = ((), (), s32[]{:S(2)}) async-start(), calls=%async_computation.2 | async-start | bytes 4456448 | tf_op jit(solution)/shard_map/all_gather | solution.py:232
  8.1 121.6 %all-gather.5.cloned.1.call-start = ((), (), s32[]{:S(2)}) async-start(), calls=%async_computation | async-start | bytes 4456448 | tf_op jit(solution)/shard_map/all_gather | solution.py:233
  8.9 156.8 %all-gather.11.cloned.1.call-start = ((), (), s32[]{:S(2)}) async-start(), calls=%async_computation.3 | async-start | bytes 2228224 | tf_op jit(solution)/shard_map/all_gather | solution.py:234
  96.7 38.6 %copy-start.4 = (bf16[1,512,1024]{2,1,0:T(8,128)(2,1)S(1)}, bf16[1,512,1024]{2,1,0:T(8,128)(2,1)}, u32[]{:S(2)}) copy-start(bf16[1,512,1024]{2,1,0:T(8,128)(2,1)} %param.10) | copy-start | bytes 3145732
  135.3 2.7 copy-start.2
  137.9 2.7 copy-start.3
  140.6 2.7 copy-start.6
  169.0 36.8 %copy-start.1 = (bf16[512,1024]{1,0:T(8,128)(2,1)}, bf16[512,1024]{1,0:T(8,128)(2,1)S(1)}, u32[]{:S(2)}) copy-start(bf16[512,1024]{1,0:T(8,128)(2,1)S(1)} %get-tuple-element.8.h_ref) | copy-start | bytes 3145732
Sparse Core Ops, SparseCore 0:
  9.0 43.6 all-gather.6
  54.3 36.8 all-gather.8
  92.8 36.8 all-gather.4
  131.2 34.4 all-gather.10

commit v2 on v1

--- a/solution.py
+++ b/solution.py
@@ -16,31 +16,188 @@
     return wide * lax.rsqrt(jnp.mean(wide * wide, axis=-1, keepdims=True) + EPS)
 
 
-def attention_layer(tokens, w_query, w_key, w_value, w_out):
-    seq_count = tokens.shape[0]
-    seq_len = tokens.shape[1]
-    head_dim = w_query.shape[2]
-    normed = rms_norm(tokens).astype(jnp.bfloat16)
-    query = jnp.einsum('bsd,dhk->bshk', normed, w_query, preferred_element_type=jnp.float32).astype(jnp.bfloat16)
-    keys = jnp.einsum('bsd,dhk->bshk', normed, w_key, preferred_element_type=jnp.float32).astype(jnp.bfloat16)
-    values = jnp.einsum('bsd,dhk->bshk', normed, w_value, preferred_element_type=jnp.float32).astype(jnp.bfloat16)
-    scores = jnp.einsum('bqhk,bshk->bhqs', query, keys, preferred_element_type=jnp.float32) * head_dim ** -0.5
-    causal = lax.broadcasted_iota(jnp.int32, (seq_len, seq_len), 0) >= lax.broadcasted_iota(jnp.int32, (seq_len, seq_len), 1)
-    attn_weights = jax.nn.softmax(jnp.where(causal, scores, -jnp.inf), axis=-1).astype(jnp.bfloat16)
-    context = jnp.einsum('bhqs,bshk->bqhk', attn_weights, values, preferred_element_type=jnp.float32).astype(jnp.bfloat16)
-    attn_out = jnp.einsum('crd,de->cre', context.reshape(seq_count, seq_len, -1), w_out, preferred_element_type=jnp.float32)
-    return (tokens.astype(jnp.float32) + attn_out).astype(jnp.bfloat16)
-
-
-def router_gates(hidden, w_router, expert_ids):
-    normed = rms_norm(hidden)
-    logits = jnp.dot(normed, w_router, precision=lax.Precision.HIGHEST, preferred_element_type=jnp.float32)
-    chosen = jnp.take_along_axis(logits, expert_ids, axis=-1)
-    gates = jax.nn.softmax(chosen, axis=-1)
-    experts = w_router.shape[1]
-    match = expert_ids[:, :, None] == jnp.arange(experts, dtype=jnp.int32)
-    dense = jnp.sum(jnp.where(match, gates[:, :, None], 0.0), axis=1)
-    return normed.astype(jnp.bfloat16), dense.T
+def attend_pair(q_ref, k_ref, v_ref, c_ref, i, scale):
+    seq, lanes = q_ref.shape[0], 128
+    cols = pl.ds(pl.multiple_of(i * lanes, lanes), lanes)
+    step = seq // 2
+    lane = lax.broadcasted_iota(jnp.int32, (1, lanes), 1)
+    keep = [jnp.where(lane < lanes // 2, 1.0, 0.0).astype(jnp.bfloat16), jnp.where(lane < lanes // 2, 0.0, 1.0).astype(jnp.bfloat16)]
+    for b in range(2):
+        rows, keys = slice(b * step, (b + 1) * step), (b + 1) * step
+        q, k, v = q_ref[rows, cols], k_ref[:keys, cols], v_ref[:keys, cols]
+        causal = (lax.broadcasted_iota(jnp.int32, (step, keys), 0) + b * step) >= lax.broadcasted_iota(jnp.int32, (step, keys), 1)
+        context = None
+        for side in range(2):
+            s = lax.dot_general(q * keep[side], k, (((1,), (1,)), ((), ())), preferred_element_type=jnp.float32) * scale
+            s = jnp.where(causal, s, -jnp.inf)
+            e = jnp.exp(s - jnp.max(s, axis=-1, keepdims=True))
+            p = (e * (1.0 / jnp.sum(e, axis=-1, keepdims=True))).astype(jnp.bfloat16)
+            c = jnp.dot(p, v * keep[side], preferred_element_type=jnp.float32)
+            context = c if context is None else context + c
+        c_ref[rows, cols] = context.astype(jnp.bfloat16)
+
+
+def front_kernel(n, head_dim, x_ref, wq_hbm, wk_hbm, wv_hbm, wo_hbm, wr_ref, ids_ref, h_ref, u_ref, g_ref,
+                 wbuf, nbuf, qkv, cbuf, r_send, r_recv, d_send, d_recv, loc, *, lag):
+    me = lax.axis_index('ep')
+    pos, core = lax.div(me, 2), lax.rem(me, 2)
+    share = wq_hbm.shape[0]
+    half = share // 2
+    mats = 4
+
+    def peer(z):
+        return {'ep': lax.rem(z + n, n) * 2 + core}
+
+    sibling = {'ep': pos * 2 + (1 - core)}
+    barrier = pltpu.get_barrier_semaphore()
+    for who in (peer(pos + 1), peer(pos - 1), sibling):
+        pl.semaphore_signal(barrier, inc=1, device_id=who, device_id_type=MESH)
+
+    def block(d, s):
+        origin = lax.rem(pos + (n - s if d == 0 else s), n) * 2 + core
+        return pl.ds(pl.multiple_of(origin * share + d * half, half), half)
+
+    def ring(d, s, m):
+        rows = block(d, s)
+        return pltpu.make_async_remote_copy(
+            src_ref=wbuf.at[m, rows], dst_ref=wbuf.at[m, rows], send_sem=r_send.at[d, s, m], recv_sem=r_recv.at[d, s, m],
+            device_id=peer(pos + (1 if d == 0 else n - 1)), device_id_type=MESH)
+
+    def across(d, s, m):
+        rows = block(d, s)
+        return pltpu.make_async_remote_copy(
+            src_ref=wbuf.at[m, rows], dst_ref=wbuf.at[m, rows], send_sem=d_send.at[d, s, m], recv_sem=d_recv.at[d, s, m],
+            device_id=sibling, device_id_type=MESH)
+
+    loads = []
+    for m, src in enumerate((wq_hbm, wk_hbm, wv_hbm, wo_hbm)):
+        loads.append(pltpu.make_async_copy(src, wbuf.at[m, pl.ds(pl.multiple_of(me * share, share), share)], loc.at[m]))
+        loads[-1].start()
+    pl.semaphore_wait(barrier, 3)
+    for m in range(3):
+        loads[m].wait()
+        for d in range(2):
+            ring(d, 0, m).start()
+    loads[3].wait()
+    for m in range(mats):
+        for d in range(2):
+            across(d, 0, m).start()
+    nbuf[...] = rms_norm(x_ref[...]).astype(jnp.bfloat16)
+
+    def relay(s, m):
+        for d in range(2):
+            ring(d, s - 1, m).wait_recv()
+
+            @pl.when(s < n - 1)
+            def _():
+                ring(d, s, m).start()
+
+            across(d, s, m).start()
+
+    def gather(s, _):
+        for m in range(3):
+            relay(s, m)
+
+        @pl.when(s == lag)
+        def _():
+            for d in range(2):
+                ring(d, 0, 3).start()
+
+        @pl.when(s > lag)
+        def _():
+            relay(s - lag, 3)
+
+        return 0
+
+    lax.fori_loop(1, n, gather, 0)
+
+    def settle(m0, m1):
+        def go(s, _):
+            for m in range(m0, m1):
+                for d in range(2):
+                    across(d, s, m).wait_recv()
+            return 0
+        lax.fori_loop(0, n, go, 0)
+
+    settle(0, 3)
+    width = nbuf.shape[1] // 2
+
+    def project(j, _):
+        m, c = lax.div(j, 2), lax.rem(j, 2)
+        cols = pl.ds(pl.multiple_of(c * width, width), width)
+        qkv[m, :, cols] = jnp.dot(nbuf[...], wbuf[m, :, cols], preferred_element_type=jnp.float32).astype(jnp.bfloat16)
+        return 0
+
+    lax.fori_loop(0, 6, project, 0)
+
+    pairs = nbuf.shape[1] // 128
+    left = lag
+
+    def heads(i, _):
+        attend_pair(qkv.at[0], qkv.at[1], qkv.at[2], cbuf, i, head_dim ** -0.5)
+
+        @pl.when(i < left)
+        def _():
+            relay(n - lag + i, 3)
+        return 0
+
+    lax.fori_loop(0, pairs, heads, 0)
+    settle(3, 4)
+    for j in range(2):
+        cols = slice(j * width, (j + 1) * width)
+        mixed = jnp.dot(cbuf[...], wbuf[3, :, cols], preferred_element_type=jnp.float32)
+        h_ref[:, cols] = (x_ref[:, cols].astype(jnp.float32) + mixed).astype(jnp.bfloat16)
+    z = rms_norm(h_ref[...])
+    u_ref[...] = z.astype(jnp.bfloat16)
+    logits = lax.dot_general(wr_ref[...], z, (((1,), (1,)), ((), ())), precision=lax.Precision.HIGHEST, preferred_element_type=jnp.float32)
+    expert = lax.broadcasted_iota(jnp.int32, logits.shape, 0)
+    match = expert == ids_ref[0:1, :]
+    for j in range(1, ids_ref.shape[0]):
+        match = match | (expert == ids_ref[j:j + 1, :])
+    logits = jnp.where(match, logits, -jnp.inf)
+    e = jnp.where(match, jnp.exp(logits - jnp.max(logits, axis=0, keepdims=True)), 0.0)
+    gates = e / jnp.sum(e, axis=0, keepdims=True)
+    classes, rows = g_ref.shape[0], g_ref.shape[1]
+    per = gates.shape[0] // n
+    for c in range(classes):
+        taken = [gates[(c + r * classes) * per:(c + r * classes + 1) * per] for r in range(n // classes)]
+        if n // classes * per < rows:
+            taken.append(jnp.zeros((rows - n // classes * per, gates.shape[1]), jnp.float32))
+        g_ref[c] = jnp.concatenate(taken, axis=0)
+
+    def drain(s, _):
+        for m in range(mats):
+            for d in range(2):
+                across(d, s, m).wait_send()
+
+                @pl.when(s < n - 1)
+                def _():
+                    ring(d, s, m).wait_send()
+        return 0
+
+    lax.fori_loop(0, n, drain, 0)
+
+
+def front(x, w_query, w_key, w_value, w_out, w_router_t, ids_t, n, classes, head_dim):
+    tok, dim = x.shape
+    dma = pltpu.SemaphoreType.DMA
+    any_spec = pl.BlockSpec(memory_space=pl.ANY)
+    vmem = pl.BlockSpec(memory_space=pltpu.VMEM)
+    return pl.pallas_call(
+        functools.partial(front_kernel, n, head_dim, lag=3),
+        out_shape=[jax.ShapeDtypeStruct((tok, dim), jnp.bfloat16), jax.ShapeDtypeStruct((tok, dim), jnp.bfloat16), jax.ShapeDtypeStruct((classes, 8, tok), jnp.float32)],
+        in_specs=[vmem, any_spec, any_spec, any_spec, any_spec, vmem, vmem],
+        out_specs=[vmem, vmem, vmem],
+        scratch_shapes=[
+            pltpu.VMEM((4, dim, dim), jnp.bfloat16),
+            pltpu.VMEM((tok, dim), jnp.bfloat16),
+            pltpu.VMEM((3, tok, dim), jnp.bfloat16),
+            pltpu.VMEM((tok, dim), jnp.bfloat16),
+            dma((2, n, 4)), dma((2, n, 4)), dma((2, n, 4)), dma((2, n, 4)), dma((4,)),
+        ],
+        compiler_params=pltpu.CompilerParams(collective_id=2, has_side_effects=True, vmem_limit_bytes=60_000_000),
+        name='attention_front',
+    )(x, w_query, w_key, w_value, w_out, w_router_t, ids_t)
 
 
 def moe_kernel(n, hops, u_hbm, g_ref, h_ref, w1_hbm, w3_hbm, w2_hbm, y_ref,
@@ -228,16 +385,10 @@
     n = mesh.shape['ep'] // 2
 
     def local_layer(tokens, w_query, w_key, w_value, w_out, w_router, w_one, w_three, w_two, expert_ids):
-        full_query = lax.all_gather(w_query, 'ep', axis=0, tiled=True)
-        full_key = lax.all_gather(w_key, 'ep', axis=0, tiled=True)
-        full_value = lax.all_gather(w_value, 'ep', axis=0, tiled=True)
-        full_out = lax.all_gather(w_out, 'ep', axis=0, tiled=True)
-        hidden = attention_layer(tokens, full_query, full_key, full_value, full_out)
         tok, dim = tokens.shape[0] * tokens.shape[1], tokens.shape[2]
-        hidden = hidden.reshape(tok, dim)
-        u, gates = router_gates(hidden, w_router, expert_ids.reshape(tok, -1))
-        per = gates.shape[0] // n
-        gates = jnp.pad(gates.reshape(n, per, tok), ((0, 0), (0, 8 - per), (0, 0)))
+        flat = [w.reshape(w.shape[0], -1) for w in (w_query, w_key, w_value)]
+        ids_t = expert_ids.reshape(tok, -1).T
+        hidden, u, gates = front(tokens.reshape(tok, dim), *flat, w_out, w_router.T, ids_t, n, n, w_query.shape[2])
         out = moe(u, gates, hidden, w_one, w_three, w_two, n, n - 1)
         return out.reshape(tokens.shape)
 

time: 483 us -> 342 us (0.71)
  waiting for transfers between devices: 113 us -> 0 us
  Pallas kernels: 266 us -> 331 us
  local copies, waits for them, and re-layouts: 52.2 us -> 7.69 us
  matrix products: 33.2 us -> 0 us
  between operations: 13.3 us -> 0.02 us
    all_gather x4 -> x0, waiting for transfers between devices: 110 us -> none  [the longest x1 40.5 us: local_layer(): full_query = lax.all_gather(w_query, 'ep', axis=0, tiled=True)]
    pallas_call x0 -> x1, Pallas kernels: none -> 71.6 us  [front(): pl.pallas_call(functools.partial(front_kernel, n, head_dim, lag=3), out_s...]
    gather x5 -> x0, local copies, waits for them, and re-layouts: 33.7 us -> none  [router_gates(): chosen = jnp.take_along_axis(logits, expert_ids, axis=-1)]
    all_gather x3 -> x0, local copies, waits for them, and re-layouts: 15.5 us -> none  [the longest x1 5.51 us: local_layer(): full_value = lax.all_gather(w_value, 'ep', axis=0, tiled=True)]
    dot_general x3 -> x0, matrix products: 14.5 us -> none  [the longest x1 8.95 us: attention_layer(): jnp.einsum('bhqs,bshk->bqhk', attn_weights, values, preferred_element_typ...]
    sub x1 -> x0, matrix products: 10.7 us -> none  [attention_layer(): jax.nn.softmax(jnp.where(causal, scores, -jnp.inf), axis=-1)]
    unnamed x3 -> x0, matrix products: 8.05 us -> none
    pallas_call x1, Pallas kernels: 266 us -> 259 us  [moe(): pl.pallas_call(functools.partial(moe_kernel, n, hops, pieces_u=pieces_u,...]
  transfers between devices with their start and end apart: 4 -> 0, of which waited for: 4 -> 0; matrix products, arithmetic and copies ran while one was open for 10% -> 0% of each run, Pallas kernels for 0% -> 0%
where the time goes in v2:
time: 342 us; the launch traced here: 339 us
  Pallas kernels  331 us (97%)
  local copies, waits for them, and re-layouts  7.69 us (2%)
    pallas_call x1, Pallas kernels, moe(): pl.pallas_call(functools.partial(moe_kernel, n, hops, pieces_u=pieces_u,...  259 us
    pallas_call x1, Pallas kernels, front(): pl.pallas_call(functools.partial(front_kernel, n, head_dim, lag=3), out_s...  71.6 us

profile of v2, /device:TPU:21, one launch (start us, length us, event | category | flops | bytes accessed | tf_op | source)
XLA Modules:
  0.0 338.5 jit_solution(4336642649018534009)
XLA Ops:
  0.0 1.8 reshape.19.wq_hbm
  1.8 1.8 reshape.20.wk_hbm
  3.6 1.8 reshape.21.wv_hbm
  5.4 71.6 %attention_front.1 = (bf16[512,1024]{1,0:T(8,128)(2,1)}, bf16[512,1024]{1,0:T(8,128)(2,1)}, f32[8,8,512]{2,1,0:T(8,128)}) custom-call(bf16[512,1024]{1,0:T(8,128)(2,1)} %bitcast.7, bf16[64,1024]{1,0:T(8,128)(2,1)} %reshape.19.wq_hbm, bf16[64,1024]{1,0:T(8,128)(2,1)} %reshape.20.wk_hbm, bf16[64,1024]{1,0:T(8,128)(2,1)} %reshape.21.wv_hbm, ...), custom_call_target="tpu_custom_call" | custom-call | tf_op jit(solution)/shard_map/attention_front/pallas_call | solution.py:186
  77.1 259.2 %moe_ring.1 = bf16[512,1024]{1,0:T(8,128)(2,1)} custom-call(bf16[512,1024]{1,0:T(8,128)(2,1)} %get-tuple-element.8.u_hbm, f32[8,8,512]{2,1,0:T(8,128)} %get-tuple-element.9.g_ref, bf16[512,1024]{1,0:T(8,128)(2,1)} %get-tuple-element.10.h_ref, bf16[2,1024,512]{2,1,0:T(8,128)(2,1)} %w1_hbm.1, bf16[2,1024,512]{2,1,0:T(8,128)(2,1)} %w3_hbm.1, ...), custom_call_target="tpu_custom_call" | custom-call | tf_op jit(solution)/shard_map/moe_ring/pallas_call | solution.py:359
  336.2 2.3 copy.12

commit v3 on v2

--- a/solution.py
+++ b/solution.py
@@ -37,8 +37,10 @@
         c_ref[rows, cols] = context.astype(jnp.bfloat16)
 
 
-def front_kernel(n, head_dim, x_ref, wq_hbm, wk_hbm, wv_hbm, wo_hbm, wr_ref, ids_ref, h_ref, u_ref, g_ref,
-                 wbuf, nbuf, qkv, cbuf, r_send, r_recv, d_send, d_recv, loc, *, lag):
+def front_kernel(n, groups, head_dim, x_ref, wq_hbm, wk_hbm, wv_hbm, wo_hbm, wr_ref, ids_ref, e1_hbm, e3_hbm, e2_hbm,
+                 h_ref, u_ref, g_ref, f1_hbm, f3_hbm, f2_hbm,
+                 wbuf, nbuf, qkv, cbuf, mid1, mid3, mid2, r_send, r_recv, d_send, d_recv, loc,
+                 s1_send, s1_recv, s2_send, s2_recv, s3_send, s3_recv, *, lag):
     me = lax.axis_index('ep')
     pos, core = lax.div(me, 2), lax.rem(me, 2)
     share = wq_hbm.shape[0]
@@ -50,8 +52,50 @@
 
     sibling = {'ep': pos * 2 + (1 - core)}
     barrier = pltpu.get_barrier_semaphore()
-    for who in (peer(pos + 1), peer(pos - 1), sibling):
+    for who in (peer(pos + 1), peer(pos + n - 1), peer(pos + 2), peer(pos + n - 2), sibling):
         pl.semaphore_signal(barrier, inc=1, device_id=who, device_id_type=MESH)
+    group = lax.axis_index('dp')
+
+    def other(j):
+        return {'dp': lax.rem(group + j, groups)}
+
+    def greet(j, _):
+        pl.semaphore_signal(barrier, inc=1, device_id=other(j), device_id_type=MESH)
+        return 0
+
+    lax.fori_loop(1, groups, greet, 0)
+    far = ((e1_hbm, mid1, f1_hbm), (e3_hbm, mid3, f3_hbm), (e2_hbm, mid2, f2_hbm))
+
+    def part_rows(t, d):
+        size = far[t][0].shape[1] // (2 * groups)
+        return pl.ds(pl.multiple_of((group * 2 + d) * size, size), size)
+
+    def stage(t, d, k):
+        own, mid, out = far[t]
+        rows = part_rows(t, d)
+        two = peer(pos + (2 if d == 0 else n - 2))
+        if k == 1:
+            return pltpu.make_async_remote_copy(src_ref=own.at[:, rows], dst_ref=mid.at[d], send_sem=s1_send.at[t, d], recv_sem=s1_recv.at[t, d], device_id=two, device_id_type=MESH)
+        return pltpu.make_async_remote_copy(src_ref=mid.at[d], dst_ref=out.at[:, rows], send_sem=s2_send.at[t, d], recv_sem=s2_recv.at[t, d], device_id=two, device_id_type=MESH)
+
+    def spread(t, d, j):
+        out, rows = far[t][2], part_rows(t, d)
+        return pltpu.make_async_remote_copy(src_ref=out.at[:, rows], dst_ref=out.at[:, rows], send_sem=s3_send.at[t, d, j - 1], recv_sem=s3_recv.at[t, d, j - 1], device_id=other(j), device_id_type=MESH)
+
+    def onward(t):
+        for d in range(2):
+            stage(t, d, 1).wait_recv()
+            stage(t, d, 2).start()
+
+    def share_out(t):
+        for d in range(2):
+            stage(t, d, 2).wait_recv()
+
+            def send(j, _):
+                spread(t, d, j).start()
+                return 0
+
+            lax.fori_loop(1, groups, send, 0)
 
     def block(d, s):
         origin = lax.rem(pos + (n - s if d == 0 else s), n) * 2 + core
@@ -73,7 +117,7 @@
     for m, src in enumerate((wq_hbm, wk_hbm, wv_hbm, wo_hbm)):
         loads.append(pltpu.make_async_copy(src, wbuf.at[m, pl.ds(pl.multiple_of(me * share, share), share)], loc.at[m]))
         loads[-1].start()
-    pl.semaphore_wait(barrier, 3)
+    pl.semaphore_wait(barrier, 4 + groups)
     for m in range(3):
         loads[m].wait()
         for d in range(2):
@@ -119,6 +163,9 @@
             return 0
         lax.fori_loop(0, n, go, 0)
 
+    for t in range(3):
+        for d in range(2):
+            stage(t, d, 1).start()
     settle(0, 3)
     width = nbuf.shape[1] // 2
 
@@ -139,10 +186,15 @@
         @pl.when(i < left)
         def _():
             relay(n - lag + i, 3)
+
+        @pl.when(i == pairs // 2)
+        def _():
+            onward(0)
         return 0
 
     lax.fori_loop(0, pairs, heads, 0)
     settle(3, 4)
+    onward(1)
     for j in range(2):
         cols = slice(j * width, (j + 1) * width)
         mixed = jnp.dot(cbuf[...], wbuf[3, :, cols], preferred_element_type=jnp.float32)
@@ -164,6 +216,21 @@
         if n // classes * per < rows:
             taken.append(jnp.zeros((rows - n // classes * per, gates.shape[1]), jnp.float32))
         g_ref[c] = jnp.concatenate(taken, axis=0)
+    onward(2)
+    for t in range(3):
+        share_out(t)
+
+    def finish(j, _):
+        for t in range(3):
+            for d in range(2):
+                spread(t, d, j).wait()
+        return 0
+
+    lax.fori_loop(1, groups, finish, 0)
+    for t in range(3):
+        for d in range(2):
+            stage(t, d, 1).wait_send()
+            stage(t, d, 2).wait_send()
 
     def drain(s, _):
         for m in range(mats):
@@ -178,37 +245,42 @@
     lax.fori_loop(0, n, drain, 0)
 
 
-def front(x, w_query, w_key, w_value, w_out, w_router_t, ids_t, n, classes, head_dim):
+def front(x, w_query, w_key, w_value, w_out, w_router_t, ids_t, w_one, w_three, w_two, n, groups, classes, head_dim):
     tok, dim = x.shape
     dma = pltpu.SemaphoreType.DMA
     any_spec = pl.BlockSpec(memory_space=pl.ANY)
     vmem = pl.BlockSpec(memory_space=pltpu.VMEM)
     return pl.pallas_call(
-        functools.partial(front_kernel, n, head_dim, lag=3),
-        out_shape=[jax.ShapeDtypeStruct((tok, dim), jnp.bfloat16), jax.ShapeDtypeStruct((tok, dim), jnp.bfloat16), jax.ShapeDtypeStruct((classes, 8, tok), jnp.float32)],
-        in_specs=[vmem, any_spec, any_spec, any_spec, any_spec, vmem, vmem],
-        out_specs=[vmem, vmem, vmem],
+        functools.partial(front_kernel, n, groups, head_dim, lag=3),
+        out_shape=[jax.ShapeDtypeStruct((tok, dim), jnp.bfloat16), jax.ShapeDtypeStruct((tok, dim), jnp.bfloat16), jax.ShapeDtypeStruct((classes, 8, tok), jnp.float32),
+                   *(jax.ShapeDtypeStruct(w.shape, w.dtype) for w in (w_one, w_three, w_two))],
+        in_specs=[vmem, any_spec, any_spec, any_spec, any_spec, vmem, vmem, any_spec, any_spec, any_spec],
+        out_specs=[vmem, vmem, vmem, any_spec, any_spec, any_spec],
         scratch_shapes=[
             pltpu.VMEM((4, dim, dim), jnp.bfloat16),
             pltpu.VMEM((tok, dim), jnp.bfloat16),
             pltpu.VMEM((3, tok, dim), jnp.bfloat16),
             pltpu.VMEM((tok, dim), jnp.bfloat16),
+            *(pltpu.VMEM((2, w.shape[0], w.shape[1] // (2 * groups), w.shape[2]), jnp.bfloat16) for w in (w_one, w_three, w_two)),
             dma((2, n, 4)), dma((2, n, 4)), dma((2, n, 4)), dma((2, n, 4)), dma((4,)),
+            dma((3, 2)), dma((3, 2)), dma((3, 2)), dma((3, 2)), dma((3, 2, groups - 1)), dma((3, 2, groups - 1)),
         ],
         compiler_params=pltpu.CompilerParams(collective_id=2, has_side_effects=True, vmem_limit_bytes=60_000_000),
         name='attention_front',
-    )(x, w_query, w_key, w_value, w_out, w_router_t, ids_t)
-
-
-def moe_kernel(n, hops, u_hbm, g_ref, h_ref, w1_hbm, w3_hbm, w2_hbm, y_ref,
+    )(x, w_query, w_key, w_value, w_out, w_router_t, ids_t, w_one, w_three, w_two)
+
+
+def moe_kernel(n, hops, u_hbm, g_ref, h_ref, w1_hbm, w3_hbm, w2_hbm, f1_hbm, f3_hbm, f2_hbm, y_ref,
                ubuf, gbuf, part, acc, w1, w3, w2,
                u_send, u_recv, a_send, a_recv, g_send, g_recv, w_send, w_recv, w_loc, u_loc, *, pieces_u, pieces_a):
     me = lax.axis_index('ep')
     pos, core = lax.div(me, 2), lax.rem(me, 2)
-    tok, half = ubuf.shape[1], ubuf.shape[1] // 2
+    tok = ubuf.shape[1]
     own = w1_hbm.shape[0]
-    total = w1.shape[0]
-    ru, ra = half // pieces_u, half // pieces_a
+    classes = g_ref.shape[0]
+    ru = tok // (2 * pieces_u)
+    per = pieces_a // pieces_u
+    ra = ru // per
 
     def peer(z):
         return {'ep': lax.rem(z + 2 * n, n) * 2 + core}
@@ -216,142 +288,151 @@
     sibling = {'ep': pos * 2 + (1 - core)}
 
     barrier = pltpu.get_barrier_semaphore()
-    for k in range(1, n):
+    for k in range(1, hops + 1):
         pl.semaphore_signal(barrier, inc=1, device_id=peer(pos + k), device_id_type=MESH)
+        pl.semaphore_signal(barrier, inc=1, device_id=peer(pos + n - k), device_id_type=MESH)
     pl.semaphore_signal(barrier, inc=1, device_id=sibling, device_id_type=MESH)
 
     own_copy = pltpu.make_async_copy(u_hbm, ubuf.at[0], u_loc.at[0])
     own_copy.start()
-    mine = pl.ds(core * own, own)
-    loads = []
-    for i, (src, dst) in enumerate(((w1_hbm, w1), (w3_hbm, w3), (w2_hbm, w2))):
-        loads.append(pltpu.make_async_copy(src, dst.at[mine], w_loc.at[i]))
-        loads[-1].start()
-    pl.semaphore_wait(barrier, n)
+    near, away = lax.div(pos, classes) * 2 * own, (1 - lax.div(pos, classes)) * 2 * own
+    base = [near + core * own, away + core * own, near + (1 - core) * own, away + (1 - core) * own]
+    mats = ((w1_hbm, f1_hbm, w1), (w3_hbm, f3_hbm, w3), (w2_hbm, f2_hbm, w2))
+
+    def load(r, i):
+        return pltpu.make_async_copy(mats[i][r], mats[i][2].at[pl.ds(base[r], own)], w_loc.at[r, i])
+
+    def hand(r, i):
+        return pltpu.make_async_remote_copy(
+            src_ref=mats[i][r], dst_ref=mats[i][2].at[pl.ds(base[r], own)], send_sem=w_send.at[r, i], recv_sem=w_recv.at[r, i],
+            device_id=sibling, device_id_type=MESH)
+
+    for r in range(2):
+        for i in range(3):
+            load(r, i).start()
+    pl.semaphore_wait(barrier, 2 * hops + 1)
 
     def u_copy(d, s, p):
-        rows = pl.ds(d * half + p * ru, ru)
+        rows = pl.ds((2 * p + d) * ru, ru)
         return pltpu.make_async_remote_copy(
             src_ref=ubuf.at[s, rows], dst_ref=ubuf.at[s + 1, rows],
             send_sem=u_send.at[d, s, p], recv_sem=u_recv.at[d, s, p],
             device_id=peer(pos + (1 if d == 0 else n - 1)), device_id_type=MESH)
 
+    def a_rows(d, p):
+        return pl.ds((2 * (p // per) + d) * ru + (p % per) * ra, ra)
+
     def a_copy(d, s, p):
-        rows = pl.ds(d * half + p * ra, ra)
+        rows = a_rows(d, p)
         return pltpu.make_async_remote_copy(
             src_ref=part.at[s, rows], dst_ref=acc.at[s - 1, rows],
             send_sem=a_send.at[d, s - 1, p], recv_sem=a_recv.at[d, s - 1, p],
             device_id=peer(pos + (n - 1 if d == 0 else 1)), device_id_type=MESH)
 
     def g_copy(d, s):
-        cols = pl.ds(d * half, half)
         target = pos + (s if d == 0 else n - s)
         return pltpu.make_async_remote_copy(
-            src_ref=g_ref.at[lax.rem(target, g_ref.shape[0]), :, cols], dst_ref=gbuf.at[s - 1, :, cols],
+            src_ref=g_ref.at[lax.rem(target, classes)], dst_ref=gbuf.at[d, s - 1],
             send_sem=g_send.at[d, s - 1], recv_sem=g_recv.at[d, s - 1],
             device_id=peer(target), device_id_type=MESH)
 
-    def w_copy(i, src, dst):
-        return pltpu.make_async_remote_copy(
-            src_ref=src, dst_ref=dst.at[mine], send_sem=w_send.at[i], recv_sem=w_recv.at[i],
-            device_id=sibling, device_id_type=MESH)
-
     own_copy.wait()
     for p in range(pieces_u):
         for d in range(2):
             u_copy(d, 0, p).start()
-    w_copies = [w_copy(i, s, t) for i, (s, t) in enumerate(((w1_hbm, w1), (w3_hbm, w3), (w2_hbm, w2)))]
-    for c in w_copies:
-        c.start()
+    for r in range(2):
+        for i in range(3):
+            hand(r, i).start()
     for s in range(1, hops + 1):
         for d in range(2):
             g_copy(d, s).start()
 
-    def experts(s, gates_t, first, count):
-        gates = gates_t.T
-
-        def one(e, _):
+    def experts(s, gates, first, count, start, rows):
+        here = slice(start, start + rows)
+        gates = gates.T[here]
+
+        def one(e, fresh):
+            turn = lax.div(e, own)
+            slot = jnp.where(turn == 0, base[0], jnp.where(turn == 1, base[1], jnp.where(turn == 2, base[2], base[3]))) + lax.rem(e, own)
             lane = lax.broadcasted_iota(jnp.int32, gates.shape, 1)
-            g = jnp.sum(jnp.where(lane == e, gates, 0.0), axis=1, keepdims=True)
-            x = ubuf[s]
-            f1 = jnp.dot(x, w1[e], preferred_element_type=jnp.float32)
-            f3 = jnp.dot(x, w3[e], preferred_element_type=jnp.float32)
+            g = jnp.sum(jnp.where(lane == slot, gates, 0.0), axis=1, keepdims=True)
+            x = ubuf[s, here]
+            f1 = jnp.dot(x, w1[slot], preferred_element_type=jnp.float32)
+            f3 = jnp.dot(x, w3[slot], preferred_element_type=jnp.float32)
             a = (f1 * jax.nn.sigmoid(f1) * f3).astype(jnp.bfloat16)
             width = w2.shape[2]
             for j in range(0, width, 512):
-                o = jnp.dot(a, w2[e, :, j:j + 512], preferred_element_type=jnp.float32).astype(jnp.bfloat16).astype(jnp.float32)
-                part[s, :, j:j + 512] += jnp.where(g != 0.0, g * o, 0.0)
+                o = jnp.dot(a, w2[slot, :, j:j + 512], preferred_element_type=jnp.float32).astype(jnp.bfloat16).astype(jnp.float32)
+                part[s, here, j:j + 512] += jnp.where(g != 0.0, g * o, 0.0)
             return 0
 
         lax.fori_loop(first, first + count, one, 0)
 
-    for c in loads:
-        c.wait()
-    for c in w_copies:
-        c.wait()
+    def gates_of(s):
+        lane = lax.broadcasted_iota(jnp.int32, gbuf.shape[2:], 1)
+        return jnp.where(lax.rem(lax.div(lane, ru), 2) == 0, gbuf[0, s - 1], gbuf[1, s - 1])
+
+    def forward(s):
+        for p in range(pieces_u):
+            for d in range(2):
+                u_copy(d, s - 1, p).wait_recv()
+                if s < hops:
+                    u_copy(d, s, p).start()
+
+    for s in range(hops + 1):
+        part[s] = jnp.zeros(part.shape[1:], jnp.float32)
+    mine = g_ref[lax.rem(pos, classes)]
+    for i in range(3):
+        load(0, i).wait()
+    experts(0, mine, 0, own, 0, tok)
+    for i in range(3):
+        load(1, i).wait()
+    experts(0, mine, own, own, 0, tok)
+    forward(1)
+    for r in range(2):
+        for i in range(3):
+            hand(r, i).wait()
+    experts(0, mine, 2 * own, 2 * own, 0, tok)
     for s in range(1, hops + 1):
         for d in range(2):
             g_copy(d, s).wait()
-
-    def visit(s, _):
-        part[s] = jnp.zeros(part.shape[1:], jnp.float32)
-
-        @pl.when(s == 0)
-        def _():
-            experts(s, g_ref[lax.rem(pos, g_ref.shape[0])], 0, total)
-
-        @pl.when(s > 0)
-        def _():
-            for p in range(pieces_u):
-                for d in range(2):
-                    u_copy(d, s - 1, p).wait_recv()
-
-                    @pl.when(s < hops)
-                    def _():
-                        u_copy(d, s, p).start()
-            experts(s, gbuf[s - 1], 0, total)
-
-        return 0
-
-    lax.fori_loop(0, hops + 1, visit, 0)
-
-    def back(i, _):
-        s = hops - i
+    forward(2)
+    experts(1, gates_of(1), 0, 4 * own, 0, tok)
+    for s in range(3, hops + 1):
+        forward(s)
+    last = gates_of(hops)
+    for p in range(pieces_u):
+        experts(hops, last, 0, 4 * own, p * 2 * ru, 2 * ru)
+        for q in range(p * per, (p + 1) * per):
+            for d in range(2):
+                a_copy(d, hops, q).start()
+    for s in range(hops - 1, 1, -1):
+        experts(s, gates_of(s), 0, 4 * own, 0, tok)
+
+    for s in range(hops - 1, -1, -1):
         for p in range(pieces_a):
             for d in range(2):
-                rows = pl.ds(d * half + p * ra, ra)
-
-                @pl.when(i > 0)
-                def _():
-                    a_copy(d, s + 1, p).wait_recv()
+                rows = a_rows(d, p)
+                a_copy(d, s + 1, p).wait_recv()
+                if s > 0:
                     part[s, rows] += acc[s, rows]
-
-                @pl.when(s > 0)
-                def _():
                     a_copy(d, s, p).start()
-
-                @pl.when(s == 0)
-                def _():
-                    y_ref[rows] = (h_ref[rows].astype(jnp.float32) + part[s, rows]).astype(y_ref.dtype)
-        return 0
-
-    lax.fori_loop(0, hops + 1, back, 0)
-
-    def drain(s, _):
+                else:
+                    y_ref[rows] = (h_ref[rows].astype(jnp.float32) + (part[s, rows] + acc[s, rows])).astype(y_ref.dtype)
+
+    for s in range(hops):
         for d in range(2):
             for p in range(pieces_u):
                 u_copy(d, s, p).wait_send()
             for p in range(pieces_a):
                 a_copy(d, s + 1, p).wait_send()
-        return 0
-
-    lax.fori_loop(0, hops, drain, 0)
-
-
-def moe(u, gates, hidden, w_one, w_three, w_two, n, hops):
+
+
+def moe(u, gates, hidden, w_one, w_three, w_two, far, n):
     tok, dim = u.shape
     own, _, ff = w_one.shape
-    total = 2 * own
+    classes = gates.shape[0]
+    hops, total = classes - 1, 2 * own * (n // classes)
     pieces_u, pieces_a = 2, 4
     dma = pltpu.SemaphoreType.DMA
     any_spec = pl.BlockSpec(memory_space=pl.ANY)
@@ -359,11 +440,11 @@
     return pl.pallas_call(
         functools.partial(moe_kernel, n, hops, pieces_u=pieces_u, pieces_a=pieces_a),
         out_shape=jax.ShapeDtypeStruct((tok, dim), jnp.bfloat16),
-        in_specs=[any_spec, vmem, vmem, any_spec, any_spec, any_spec],
+        in_specs=[any_spec, vmem, vmem] + [any_spec] * 6,
         out_specs=vmem,
         scratch_shapes=[
             pltpu.VMEM((hops + 1, tok, dim), jnp.bfloat16),
-            pltpu.VMEM((hops, gates.shape[1], tok), jnp.float32),
+            pltpu.VMEM((2, hops, gates.shape[1], tok), jnp.float32),
             pltpu.VMEM((hops + 1, tok, dim), jnp.float32),
             pltpu.VMEM((hops, tok, dim), jnp.float32),
             pltpu.VMEM((total, dim, ff), jnp.bfloat16),
@@ -372,24 +453,25 @@
             dma((2, hops, pieces_u)), dma((2, hops, pieces_u)),
             dma((2, hops, pieces_a)), dma((2, hops, pieces_a)),
             dma((2, hops)), dma((2, hops)),
-            dma((3,)), dma((3,)), dma((3,)), dma((1,)),
+            dma((2, 3)), dma((2, 3)), dma((2, 3)), dma((1,)),
         ],
         compiler_params=pltpu.CompilerParams(collective_id=1, has_side_effects=True, vmem_limit_bytes=66_000_000),
         name='moe_ring',
-    )(u, gates, hidden, w_one, w_three, w_two)
+    )(u, gates, hidden, w_one, w_three, w_two, *far)
 
 
 def solution(mesh):
     tok_spec = P(('dp', 'ep'))
     row_spec = P('ep')
     n = mesh.shape['ep'] // 2
+    groups = mesh.shape['dp']
 
     def local_layer(tokens, w_query, w_key, w_value, w_out, w_router, w_one, w_three, w_two, expert_ids):
         tok, dim = tokens.shape[0] * tokens.shape[1], tokens.shape[2]
         flat = [w.reshape(w.shape[0], -1) for w in (w_query, w_key, w_value)]
         ids_t = expert_ids.reshape(tok, -1).T
-        hidden, u, gates = front(tokens.reshape(tok, dim), *flat, w_out, w_router.T, ids_t, n, n, w_query.shape[2])
-        out = moe(u, gates, hidden, w_one, w_three, w_two, n, n - 1)
+        hidden, u, gates, *far = front(tokens.reshape(tok, dim), *flat, w_out, w_router.T, ids_t, w_one, w_three, w_two, n, groups, n // 2, w_query.shape[2])
+        out = moe(u, gates, hidden, w_one, w_three, w_two, far, n)
         return out.reshape(tokens.shape)
 
     return jax.shard_map(local_layer, mesh=mesh, in_specs=(tok_spec, row_spec, row_spec, row_spec, row_spec, P(), row_spec, row_spec, row_spec, tok_spec), out_specs=tok_spec, check_vma=False)

time: 342 us -> 311 us (0.909)
  Pallas kernels: 331 us -> 303 us
    pallas_call x1, Pallas kernels: 259 us -> 132 us  [moe(): pl.pallas_call(functools.partial(moe_kernel, n, hops, pieces_u=pieces_u,...]
    pallas_call x1, Pallas kernels: 71.6 us -> 171 us  [front(): pl.pallas_call(functools.partial(front_kernel, n, groups, head_dim, lag=3...]
where the time goes in v3:
time: 311 us
  Pallas kernels  303 us (97%)
  local copies, waits for them, and re-layouts  7.7 us (2%)
    pallas_call x1, Pallas kernels, front(): pl.pallas_call(functools.partial(front_kernel, n, groups, head_dim, lag=3...  171 us
    pallas_call x1, Pallas kernels, moe(): pl.pallas_call(functools.partial(moe_kernel, n, hops, pieces_u=pieces_u,...  132 us

profile of v3, /device:TPU:21, one launch (start us, length us, event | category | flops | bytes accessed | tf_op | source)
XLA Modules:
  0.0 310.7 jit_solution(7656622885870570011)
XLA Ops:
  0.0 1.8 reshape.19.wq_hbm
  1.8 1.8 reshape.20.wk_hbm
  3.6 1.8 reshape.21.wv_hbm
  5.4 170.8 %attention_front.1 = (bf16[512,1024]{1,0:T(8,128)(2,1)}, bf16[512,1024]{1,0:T(8,128)(2,1)}, f32[4,8,512]{2,1,0:T(8,128)}, bf16[2,1024,512]{2,1,0:T(8,128)(2,1)},...) custom-call(bf16[512,1024]{1,0:T(8,128)(2,1)} %bitcast.7, bf16[64,1024]{1,0:T(8,128)(2,1)} %reshape.19.wq_hbm, ...), custom_call_target="tpu_custom_call" | custom-call | tf_op jit(solution)/shard_map/attention_front/pallas_call | solution.py:253
  176.2 132.2 %moe_ring.1 = bf16[512,1024]{1,0:T(8,128)(2,1)} custom-call(bf16[512,1024]{1,0:T(8,128)(2,1)} %get-tuple-element.11.u_hbm, f32[4,8,512]{2,1,0:T(8,128)} %get-tuple-element.12.g_ref, bf16[512,1024]{1,0:T(8,128)(2,1)} %get-tuple-element.13.h_ref, bf16[2,1024,512]{2,1,0:T(8,128)(2,1)} %w1_hbm.1, bf16[2,1024,512]{2,1,0:T(8,128)(2,1)} %w3_hbm.1, ...), custom_call_target="tpu_custom_call" | custom-call | tf_op jit(solution)/shard_map/moe_ring/pallas_call | solution.py:440
  308.5 2.3 copy.12

commit v4 on v0

v4 whole, which is shorter than its diff:
```python
import functools

import jax
import jax.numpy as jnp
from jax import lax
from jax.experimental import pallas as pl
from jax.experimental.pallas import tpu as pltpu
from jax.sharding import PartitionSpec as P

EPS = 1e-6
MESH = pl.DeviceIdType.MESH


def rms_norm(vals):
    wide = vals.astype(jnp.float32)
    return wide * lax.rsqrt(jnp.mean(wide * wide, axis=-1, keepdims=True) + EPS)


def attend_pair(q_ref, k_ref, v_ref, c_ref, i, scale):
    seq, lanes = q_ref.shape[0], 128
    cols = pl.ds(pl.multiple_of(i * lanes, lanes), lanes)
    step = seq // 2
    lane = lax.broadcasted_iota(jnp.int32, (1, lanes), 1)
    keep = [jnp.where(lane < lanes // 2, 1.0, 0.0).astype(jnp.bfloat16), jnp.where(lane < lanes // 2, 0.0, 1.0).astype(jnp.bfloat16)]
    for b in range(2):
        rows, keys = slice(b * step, (b + 1) * step), (b + 1) * step
        q, k, v = q_ref[rows, cols], k_ref[:keys, cols], v_ref[:keys, cols]
        causal = (lax.broadcasted_iota(jnp.int32, (step, keys), 0) + b * step) >= lax.broadcasted_iota(jnp.int32, (step, keys), 1)
        context = None
        for side in range(2):
            s = lax.dot_general(q * keep[side], k, (((1,), (1,)), ((), ())), preferred_element_type=jnp.float32) * scale
            s = jnp.where(causal, s, -jnp.inf)
            e = jnp.exp(s - jnp.max(s, axis=-1, keepdims=True))
            p = (e * (1.0 / jnp.sum(e, axis=-1, keepdims=True))).astype(jnp.bfloat16)
            c = jnp.dot(p, v * keep[side], preferred_element_type=jnp.float32)
            context = c if context is None else context + c
        c_ref[rows, cols] = context.astype(jnp.bfloat16)


def layer_kernel(n, groups, head_dim, x_ref, wq_hbm, wk_hbm, wv_hbm, wo_hbm, wr_ref, ids_ref, e1_hbm, e3_hbm, e2_hbm, y_ref,
                 wbuf, nbuf, qkv, ubuf, g_own, gbuf, part, acc, w1, w3, w2,
                 r_send, r_recv, d_send, d_recv, loc, w_loc, z_send, z_recv, s_send, s_recv, w_send, w_recv,
                 u_send, u_recv, a_send, a_recv, g_send, g_recv, *, pieces_u, pieces_a):
    me, group = lax.axis_index('ep'), lax.axis_index('dp')
    pos, core = lax.div(me, 2), lax.rem(me, 2)
    share = wq_hbm.shape[0]
    half = share // 2
    mats = 4
    tok, dim = x_ref.shape
    own, classes = e1_hbm.shape[0], g_own.shape[0]
    hops = classes - 1
    ru = tok // (2 * pieces_u)
    per = pieces_a // pieces_u
    ra = ru // per

    def peer(z):
        return {'ep': lax.rem(z, n) * 2 + core}

    def other(j):
        return {'dp': lax.rem(group + j, groups)}

    sibling = {'ep': pos * 2 + (1 - core)}

    def remote(src, dst, send, recv, device):
        return pltpu.make_async_remote_copy(src_ref=src, dst_ref=dst, send_sem=send, recv_sem=recv, device_id=device, device_id_type=MESH)

    barrier = pltpu.get_barrier_semaphore()

    def greet_ring(k, _):
        pl.semaphore_signal(barrier, inc=1, device_id=peer(pos + k), device_id_type=MESH)
        return 0

    def greet_groups(j, _):
        pl.semaphore_signal(barrier, inc=1, device_id=other(j), device_id_type=MESH)
        return 0

    lax.fori_loop(1, n, greet_ring, 0)
    lax.fori_loop(1, groups, greet_groups, 0)
    pl.semaphore_signal(barrier, inc=1, device_id=sibling, device_id_type=MESH)


    def block(d, s):
        origin = lax.rem(pos + (n - s if d == 0 else s), n) * 2 + core
        return pl.ds(pl.multiple_of(origin * share + d * half, half), half)

    def ring(d, s, m):
        rows = block(d, s)
        return remote(wbuf.at[m, rows], wbuf.at[m, rows], r_send.at[d, s, m], r_recv.at[d, s, m], peer(pos + (1 if d == 0 else n - 1)))

    def across(d, s, m):
        rows = block(d, s)
        return remote(wbuf.at[m, rows], wbuf.at[m, rows], d_send.at[d, s, m], d_recv.at[d, s, m], sibling)


    near, away = lax.div(pos, classes) * 2 * own, (1 - lax.div(pos, classes)) * 2 * own
    base = [near + core * own, near + (1 - core) * own, away + core * own, away + (1 - core) * own]
    experts_of = ((e1_hbm, w1), (e3_hbm, w3), (e2_hbm, w2))

    def rows_of(t, d):
        size = experts_of[t][0].shape[1] // (2 * groups)
        return pl.ds(pl.multiple_of((group * 2 + d) * size, size), size)

    def load(t):
        return pltpu.make_async_copy(experts_of[t][0], experts_of[t][1].at[pl.ds(base[0], own)], w_loc.at[t])

    def hand(r, t):
        kept = experts_of[t][1].at[pl.ds(base[2 * r], own)]
        return remote(experts_of[t][0] if r == 0 else kept, kept, w_send.at[r, t], w_recv.at[r, t], sibling)

    def fetch(t, d):
        rows = rows_of(t, d)
        return remote(experts_of[t][0].at[:, rows], experts_of[t][1].at[pl.ds(base[0], own), rows], z_send.at[t, d], z_recv.at[t, d], peer(pos + n // 2))

    def spread(t, d, j):
        piece = experts_of[t][1].at[pl.ds(base[2], own), rows_of(t, d)]
        return remote(piece, piece, s_send.at[t, d, j - 1], s_recv.at[t, d, j - 1], other(j))

    def share_out(t, d):
        fetch(t, d).wait_recv()

        def send(j, _):
            spread(t, d, j).start()
            return 0

        lax.fori_loop(1, groups, send, 0)

    def collect(t):
        def take(j, _):
            for d in range(2):
                spread(t, d, j).wait_recv()
            return 0

        lax.fori_loop(1, groups, take, 0)
        hand(1, t).start()

    shards = []
    for m, src in enumerate((wq_hbm, wk_hbm, wv_hbm, wo_hbm)):
        shards.append(pltpu.make_async_copy(src, wbuf.at[m, pl.ds(pl.multiple_of(me * share, share), share)], loc.at[m]))
        shards[-1].start()
    for t in range(3):
        load(t).start()
    pl.semaphore_wait(barrier, n + groups - 1)
    for m in range(mats):
        shards[m].wait()
        for d in range(2):
            ring(d, 0, m).start()
    for m in range(mats):
        for d in range(2):
            across(d, 0, m).start()
    for t in range(3):
        hand(0, t).start()
    nbuf[...] = rms_norm(x_ref[...]).astype(jnp.bfloat16)
    for s in range(hops + 1):
        part[s] = jnp.zeros(part.shape[1:], jnp.float32)

    def gather(s, _):
        for m in range(mats):
            for d in range(2):
                ring(d, s - 1, m).wait_recv()

                @pl.when(s < n - 1)
                def _():
                    ring(d, s, m).start()

                across(d, s, m).start()
        return 0

    lax.fori_loop(1, n, gather, 0)
    for t in range(3):
        for d in range(2):
            fetch(t, d).start()

    def settle(s, _):
        for m in range(mats):
            for d in range(2):
                across(d, s, m).wait_recv()
        return 0

    lax.fori_loop(0, n, settle, 0)
    width = dim // 2

    def project(j, _):
        m, c = lax.div(j, 2), lax.rem(j, 2)
        cols = pl.ds(pl.multiple_of(c * width, width), width)
        qkv[m, :, cols] = jnp.dot(nbuf[...], wbuf[m, :, cols], preferred_element_type=jnp.float32).astype(jnp.bfloat16)
        return 0

    lax.fori_loop(0, 6, project, 0)
    pairs = dim // 128

    def heads(i, _):
        attend_pair(qkv.at[0], qkv.at[1], qkv.at[2], nbuf, i, head_dim ** -0.5)

        @pl.when(i == pairs // 2)
        def _():
            share_out(0, 0)
        return 0

    lax.fori_loop(0, pairs, heads, 0)
    share_out(0, 1)
    for j in range(2):
        cols = slice(j * width, (j + 1) * width)
        mixed = jnp.dot(nbuf[...], wbuf[3, :, cols], preferred_element_type=jnp.float32)
        y_ref[:, cols] = (x_ref[:, cols].astype(jnp.float32) + mixed).astype(jnp.bfloat16)
    z = rms_norm(y_ref[...])
    ubuf[0] = z.astype(jnp.bfloat16)
    logits = lax.dot_general(wr_ref[...], z, (((1,), (1,)), ((), ())), precision=lax.Precision.HIGHEST, preferred_element_type=jnp.float32)
    expert = lax.broadcasted_iota(jnp.int32, logits.shape, 0)
    match = expert == ids_ref[0:1, :]
    for j in range(1, ids_ref.shape[0]):
        match = match | (expert == ids_ref[j:j + 1, :])
    logits = jnp.where(match, logits, -jnp.inf)
    e = jnp.where(match, jnp.exp(logits - jnp.max(logits, axis=0, keepdims=True)), 0.0)
    gates = e / jnp.sum(e, axis=0, keepdims=True)
    layer = gates.shape[0] // n
    for c in range(classes):
        g_own[c] = jnp.concatenate([gates[(c + r * classes) * layer:(c + r * classes + 1) * layer] for r in range(n // classes)], axis=0)


    def u_copy(d, s, p):
        rows = pl.ds((2 * p + d) * ru, ru)
        return remote(ubuf.at[s, rows], ubuf.at[s + 1, rows], u_send.at[d, s, p], u_recv.at[d, s, p], peer(pos + (1 if d == 0 else n - 1)))

    def a_rows(d, p):
        return pl.ds((2 * (p // per) + d) * ru + (p % per) * ra, ra)

    def a_copy(d, s, p):
        rows = a_rows(d, p)
        return remote(part.at[s, rows], acc.at[s - 1, rows], a_send.at[d, s - 1, p], a_recv.at[d, s - 1, p], peer(pos + (n - 1 if d == 0 else 1)))

    def g_copy(d, s):
        target = pos + (s if d == 0 else n - s)
        return remote(g_own.at[lax.rem(target, classes)], gbuf.at[d, s - 1], g_send.at[d, s - 1], g_recv.at[d, s - 1], peer(target))

    for p in range(pieces_u):
        for d in range(2):
            u_copy(d, 0, p).start()

    def experts(s, gates, first, count, start=0, rows=tok):
        here = slice(start, start + rows)
        gates = gates.T[here]

        def one(e, _):
            turn = lax.div(e, own)
            slot = jnp.where(turn == 0, base[0], jnp.where(turn == 1, base[1], jnp.where(turn == 2, base[2], base[3]))) + lax.rem(e, own)
            lane = lax.broadcasted_iota(jnp.int32, gates.shape, 1)
            g = jnp.sum(jnp.where(lane == slot, gates, 0.0), axis=1, keepdims=True)
            u = ubuf[s, here]
            f1 = jnp.dot(u, w1[slot], preferred_element_type=jnp.float32)
            f3 = jnp.dot(u, w3[slot], preferred_element_type=jnp.float32)
            a = (f1 * jax.nn.sigmoid(f1) * f3).astype(jnp.bfloat16)
            for j in range(0, dim, 512):
                o = jnp.dot(a, w2[slot, :, j:j + 512], preferred_element_type=jnp.float32).astype(jnp.bfloat16).astype(jnp.float32)
                part[s, here, j:j + 512] += jnp.where(g != 0.0, g * o, 0.0)
            return 0

        lax.fori_loop(first, first + count, one, 0)

    def gates_of(s):
        if s == 0:
            return g_own[lax.rem(pos, classes)]
        lane = lax.broadcasted_iota(jnp.int32, gbuf.shape[2:], 1)
        return jnp.where(lax.rem(lax.div(lane, ru), 2) == 0, gbuf[0, s - 1], gbuf[1, s - 1])

    def forward(s):
        for p in range(pieces_u):
            for d in range(2):
                u_copy(d, s - 1, p).wait_recv()
                if s < hops:
                    u_copy(d, s, p).start()

    for t in range(3):
        load(t).wait()
    experts(0, gates_of(0), 0, own)
    for s in range(1, hops + 1):
        for d in range(2):
            g_copy(d, s).start()
    for t in range(3):
        hand(0, t).wait()
    share_out(1, 0)
    forward(1)
    experts(0, gates_of(0), own, own)
    share_out(1, 1)
    for s in range(1, hops + 1):
        for d in range(2):
            g_copy(d, s).wait()
    experts(1, gates_of(1), 0, own)
    share_out(2, 0)
    forward(2)
    experts(1, gates_of(1), own, own)
    share_out(2, 1)
    collect(0)
    experts(2, gates_of(2), 0, 2 * own)
    for s in range(3, hops + 1):
        forward(s)
    collect(1)
    experts(hops, gates_of(hops), 0, 2 * own)
    collect(2)
    for p in range(pieces_u):
        experts(hops, gates_of(hops), 2 * own, own, p * 2 * ru, 2 * ru)
        if p == 0:
            for t in range(3):
                hand(1, t).wait_recv()
        experts(hops, gates_of(hops), 3 * own, own, p * 2 * ru, 2 * ru)
        for q in range(p * per, (p + 1) * per):
            for d in range(2):
                a_copy(d, hops, q).start()

    for s in range(hops - 1, -1, -1):
        experts(s, gates_of(s), 2 * own, 2 * own)
        for p in range(pieces_a):
            for d in range(2):
                rows = a_rows(d, p)
                a_copy(d, s + 1, p).wait_recv()
                if s > 0:
                    part[s, rows] += acc[s, rows]
                    a_copy(d, s, p).start()
                else:
                    y_ref[rows] = (y_ref[rows].astype(jnp.float32) + (part[s, rows] + acc[s, rows])).astype(y_ref.dtype)


    def drain_ring(s, _):
        for m in range(mats):
            for d in range(2):
                across(d, s, m).wait_send()

                @pl.when(s < n - 1)
                def _():
                    ring(d, s, m).wait_send()
        return 0

    lax.fori_loop(0, n, drain_ring, 0)

    def drain_groups(j, _):
        for t in range(3):
            for d in range(2):
                spread(t, d, j).wait_send()
        return 0

    lax.fori_loop(1, groups, drain_groups, 0)
    for t in range(3):
        hand(1, t).wait_send()
        for d in range(2):
            fetch(t, d).wait_send()
    for s in range(hops):
        for d in range(2):
            for p in range(pieces_u):
                u_copy(d, s, p).wait_send()
            for p in range(pieces_a):
                a_copy(d, s + 1, p).wait_send()


def layer(x, w_query, w_key, w_value, w_out, w_router_t, ids_t, w_one, w_three, w_two, n, groups, head_dim):
    tok, dim = x.shape
    own, _, ff = w_one.shape
    classes = n // 2
    hops, total = classes - 1, 4 * own
    pieces_u, pieces_a = 2, 4
    dma = pltpu.SemaphoreType.DMA
    any_spec = pl.BlockSpec(memory_space=pl.ANY)
    vmem = pl.BlockSpec(memory_space=pltpu.VMEM)
    bf16, f32 = jnp.bfloat16, jnp.float32
    return pl.pallas_call(
        functools.partial(layer_kernel, n, groups, head_dim, pieces_u=pieces_u, pieces_a=pieces_a),
        out_shape=jax.ShapeDtypeStruct((tok, dim), bf16),
        in_specs=[vmem, any_spec, any_spec, any_spec, any_spec, vmem, vmem, any_spec, any_spec, any_spec],
        out_specs=vmem,
        scratch_shapes=[
            pltpu.VMEM((4, dim, dim), bf16),
            pltpu.VMEM((tok, dim), bf16),
            pltpu.VMEM((3, tok, dim), bf16),
            pltpu.VMEM((hops + 1, tok, dim), bf16),
            pltpu.VMEM((classes, total, tok), f32),
            pltpu.VMEM((2, hops, total, tok), f32),
            pltpu.VMEM((hops + 1, tok, dim), f32),
            pltpu.VMEM((hops, tok, dim), f32),
            pltpu.VMEM((total, dim, ff), bf16),
            pltpu.VMEM((total, dim, ff), bf16),
            pltpu.VMEM((total, ff, dim), bf16),
            dma((2, n, 4)), dma((2, n, 4)), dma((2, n, 4)), dma((2, n, 4)), dma((4,)), dma((3,)),
            dma((3, 2)), dma((3, 2)), dma((3, 2, groups - 1)), dma((3, 2, groups - 1)), dma((2, 3)), dma((2, 3)),
            dma((2, hops, pieces_u)), dma((2, hops, pieces_u)),
            dma((2, hops, pieces_a)), dma((2, hops, pieces_a)),
            dma((2, hops)), dma((2, hops)),
        ],
        compiler_params=pltpu.CompilerParams(collective_id=1, has_side_effects=True, vmem_limit_bytes=67_000_000),
        name='layer_ring',
    )(x, w_query, w_key, w_value, w_out, w_router_t, ids_t, w_one, w_three, w_two)


def solution(mesh):
    tok_spec = P(('dp', 'ep'))
    row_spec = P('ep')
    n = mesh.shape['ep'] // 2
    groups = mesh.shape['dp']

    def local_layer(tokens, w_query, w_key, w_value, w_out, w_router, w_one, w_three, w_two, expert_ids):
        tok, dim = tokens.shape[0] * tokens.shape[1], tokens.shape[2]
        flat = [w.reshape(w.shape[0], -1) for w in (w_query, w_key, w_value)]
        ids_t = expert_ids.reshape(tok, -1).T
        out = layer(tokens.reshape(tok, dim), *flat, w_out, w_router.T, ids_t, w_one, w_three, w_two, n, groups, w_query.shape[2])
        return out.reshape(tokens.shape)

    return jax.shard_map(local_layer, mesh=mesh, in_specs=(tok_spec, row_spec, row_spec, row_spec, row_spec, P(), row_spec, row_spec, row_spec, tok_spec), out_specs=tok_spec, check_vma=False)
```

time: 1100 us -> 262 us (0.24); the launches traced: 1080 us -> 261 us
  waiting for transfers between devices: 418 us -> 0 us
  blocking collectives: 370 us -> 0 us
  Pallas kernels: 0 us -> 254 us
  local copies, waits for them, and re-layouts: 168 us -> 7.67 us
  matrix products: 94.2 us -> 0 us
  other arithmetic: 13.8 us -> 0 us
  between operations: 13.6 us -> 0.01 us
    all_to_all x1 -> x0, blocking collectives: 370 us -> none  [local_layer(): recv_rows = lax.all_to_all(send_rows, 'ep', 0, 1, tiled=True)]
    all_to_all x1 -> x0, waiting for transfers between devices: 309 us -> none  [local_layer(): back_rows = lax.all_to_all(done_rows, 'ep', 1, 0, tiled=True)]
    pallas_call x0 -> x1, Pallas kernels: none -> 254 us  [layer(): pl.pallas_call(functools.partial(layer_kernel, n, groups, head_dim, piece...]
    all_gather x4 -> x0, waiting for transfers between devices: 106 us -> none  [the longest x1 39.7 us: local_layer(): full_key = lax.all_gather(w_key, 'ep', axis=0, tiled=True)]
    gather x13 -> x0, local copies, waits for them, and re-layouts: 96.2 us -> none  [the longest x7 33.8 us: dispatch_tables(): slot = jnp.take_along_axis(before, ids_flat, axis=1)]
    dot_general x6 -> x0, matrix products: 73 us -> none  [the longest x1 27 us: expert_ffn(): jnp.einsum('enf,efd->end', activated, w_two, preferred_element_type=jnp.f...]
    convert_element_type x1 -> x0, local copies, waits for them, and re-layouts: 31 us -> none  [expert_ffn(): jnp.einsum('enf,efd->end', activated, w_two, preferred_element_type=jnp.f...]
    all_to_all x2 -> x0, local copies, waits for them, and re-layouts: 23.1 us -> none  [the longest x1 16.4 us: local_layer(): back_rows = lax.all_to_all(done_rows, 'ep', 1, 0, tiled=True)]
  transfers between devices with their start and end apart: 5 -> 0, of which waited for: 5 -> 0; matrix products, arithmetic and copies ran while one was open for 11% -> 0% of each run, Pallas kernels for 0% -> 0%
where the time goes in v4:
time: 262 us; the launch traced here: 261 us
  Pallas kernels  254 us (97%)
  local copies, waits for them, and re-layouts  7.67 us (3%)
    pallas_call x1, Pallas kernels, layer(): pl.pallas_call(functools.partial(layer_kernel, n, groups, head_dim, piece...  254 us
    reshape x3, local copies, waits for them, and re-layouts, local_layer(): flat = [w.reshape(w.shape[0], -1) for w in (w_query, w_key, w_value)]  5.4 us

profile of v4, /device:TPU:21, one launch (start us, length us, event | category | flops | bytes accessed | tf_op | source)
XLA Modules:
  0.0 261.5 jit_solution(12618321612731863618)
XLA Ops:
  0.0 1.8 reshape.19.wq_hbm
  1.8 1.8 reshape.20.wk_hbm
  3.6 1.8 reshape.21.wv_hbm
  5.4 253.8 %layer_ring.1 = bf16[512,1024]{1,0:T(8,128)(2,1)} custom-call(bf16[512,1024]{1,0:T(8,128)(2,1)} %bitcast.7, bf16[64,1024]{1,0:T(8,128)(2,1)} %reshape.19.wq_hbm, bf16[64,1024]{1,0:T(8,128)(2,1)} %reshape.20.wk_hbm, bf16[64,1024]{1,0:T(8,128)(2,1)} %reshape.21.wv_hbm, bf16[64,1024]{1,0:T(8,128)(2,1)} %wo_hbm.1, f32[32,1024]{1,0:T(8,128)} %bitcast.8, ...), custom_call_target="tpu_custom_call" | custom-call | tf_op jit(solution)/shard_map/layer_ring/pallas_call | solution.py:363
  259.2 2.3 copy.12

commit v5 on v4

--- a/solution.py
+++ b/solution.py
@@ -39,13 +39,12 @@
 
 def layer_kernel(n, groups, head_dim, x_ref, wq_hbm, wk_hbm, wv_hbm, wo_hbm, wr_ref, ids_ref, e1_hbm, e3_hbm, e2_hbm, y_ref,
                  wbuf, nbuf, qkv, ubuf, g_own, gbuf, part, acc, w1, w3, w2,
-                 r_send, r_recv, d_send, d_recv, loc, w_loc, z_send, z_recv, s_send, s_recv, w_send, w_recv,
+                 b_send, b_recv, c_send, c_recv, d_send, d_recv, loc, w_loc, z_send, z_recv, s_send, s_recv, w_send, w_recv,
                  u_send, u_recv, a_send, a_recv, g_send, g_recv, *, pieces_u, pieces_a):
     me, group = lax.axis_index('ep'), lax.axis_index('dp')
     pos, core = lax.div(me, 2), lax.rem(me, 2)
     share = wq_hbm.shape[0]
-    half = share // 2
-    mats = 4
+    mats = wbuf.shape[0]
     tok, dim = x_ref.shape
     own, classes = e1_hbm.shape[0], g_own.shape[0]
     hops = classes - 1
@@ -79,17 +78,29 @@
     pl.semaphore_signal(barrier, inc=1, device_id=sibling, device_id_type=MESH)
 
 
-    def block(d, s):
-        origin = lax.rem(pos + (n - s if d == 0 else s), n) * 2 + core
-        return pl.ds(pl.multiple_of(origin * share + d * half, half), half)
-
-    def ring(d, s, m):
-        rows = block(d, s)
-        return remote(wbuf.at[m, rows], wbuf.at[m, rows], r_send.at[d, s, m], r_recv.at[d, s, m], peer(pos + (1 if d == 0 else n - 1)))
-
-    def across(d, s, m):
-        rows = block(d, s)
-        return remote(wbuf.at[m, rows], wbuf.at[m, rows], d_send.at[d, s, m], d_recv.at[d, s, m], sibling)
+    parts, whole = max(1, groups // mats), max(1, mats // groups)
+    first_mat, first_row = lax.div(group * mats, groups), lax.rem(group, parts) * (share // parts)
+    order = sorted(range(n), key=lambda k: min(k, n - k))
+
+    def piece(k):
+        return wbuf.at[pl.ds(first_mat, whole), lax.rem(pos + n - k, n), core, pl.ds(pl.multiple_of(first_row, share // parts), share // parts)]
+
+    def along(k):
+        return remote(piece(0), piece(0), b_send.at[k], b_recv.at[k], peer(pos + k))
+
+    def outward(k, j):
+        return remote(piece(k), piece(k), c_send.at[k, j - 1], c_recv.at[k, j - 1], other(j))
+
+    def across(k):
+        block = wbuf.at[:, lax.rem(pos + n - k, n), core]
+        return remote(block, block, d_send.at[k], d_recv.at[k], sibling)
+
+    def each_group(do):
+        def step(j, _):
+            do(j)
+            return 0
+
+        lax.fori_loop(1, groups, step, 0)
 
 
     near, away = lax.div(pos, classes) * 2 * own, (1 - lax.div(pos, classes)) * 2 * own
@@ -135,54 +146,41 @@
 
     shards = []
     for m, src in enumerate((wq_hbm, wk_hbm, wv_hbm, wo_hbm)):
-        shards.append(pltpu.make_async_copy(src, wbuf.at[m, pl.ds(pl.multiple_of(me * share, share), share)], loc.at[m]))
+        shards.append(pltpu.make_async_copy(src, wbuf.at[m, pos, core], loc.at[m]))
         shards[-1].start()
     for t in range(3):
         load(t).start()
     pl.semaphore_wait(barrier, n + groups - 1)
     for m in range(mats):
         shards[m].wait()
-        for d in range(2):
-            ring(d, 0, m).start()
-    for m in range(mats):
-        for d in range(2):
-            across(d, 0, m).start()
+    for k in order[1:]:
+        along(k).start()
+    for t in range(3):
+        for d in range(2):
+            fetch(t, d).start()
     for t in range(3):
         hand(0, t).start()
     nbuf[...] = rms_norm(x_ref[...]).astype(jnp.bfloat16)
     for s in range(hops + 1):
         part[s] = jnp.zeros(part.shape[1:], jnp.float32)
 
-    def gather(s, _):
-        for m in range(mats):
-            for d in range(2):
-                ring(d, s - 1, m).wait_recv()
-
-                @pl.when(s < n - 1)
-                def _():
-                    ring(d, s, m).start()
-
-                across(d, s, m).start()
-        return 0
-
-    lax.fori_loop(1, n, gather, 0)
-    for t in range(3):
-        for d in range(2):
-            fetch(t, d).start()
-
-    def settle(s, _):
-        for m in range(mats):
-            for d in range(2):
-                across(d, s, m).wait_recv()
-        return 0
-
-    lax.fori_loop(0, n, settle, 0)
+    for k in order[1:]:
+        along(k).wait_recv()
+        each_group(lambda j: outward(k, j).start())
+    across(0).start()
+    for k in order[1:]:
+        each_group(lambda j: outward(k, j).wait_recv())
+        across(k).start()
+    share_out(0, 0)
+    share_out(0, 1)
+    for k in order:
+        across(k).wait_recv()
     width = dim // 2
 
     def project(j, _):
         m, c = lax.div(j, 2), lax.rem(j, 2)
         cols = pl.ds(pl.multiple_of(c * width, width), width)
-        qkv[m, :, cols] = jnp.dot(nbuf[...], wbuf[m, :, cols], preferred_element_type=jnp.float32).astype(jnp.bfloat16)
+        qkv[m, :, cols] = jnp.dot(nbuf[...], wbuf[m, :, :, :, cols].reshape(dim, width), preferred_element_type=jnp.float32).astype(jnp.bfloat16)
         return 0
 
     lax.fori_loop(0, 6, project, 0)
@@ -191,16 +189,19 @@
     def heads(i, _):
         attend_pair(qkv.at[0], qkv.at[1], qkv.at[2], nbuf, i, head_dim ** -0.5)
 
-        @pl.when(i == pairs // 2)
+        @pl.when(i == pairs // 4)
         def _():
-            share_out(0, 0)
+            share_out(1, 0)
+
+        @pl.when(i == 3 * pairs // 4)
+        def _():
+            share_out(1, 1)
         return 0
 
     lax.fori_loop(0, pairs, heads, 0)
-    share_out(0, 1)
     for j in range(2):
         cols = slice(j * width, (j + 1) * width)
-        mixed = jnp.dot(nbuf[...], wbuf[3, :, cols], preferred_element_type=jnp.float32)
+        mixed = jnp.dot(nbuf[...], wbuf[3, :, :, :, cols].reshape(dim, width), preferred_element_type=jnp.float32)
         y_ref[:, cols] = (x_ref[:, cols].astype(jnp.float32) + mixed).astype(jnp.bfloat16)
     z = rms_norm(y_ref[...])
     ubuf[0] = z.astype(jnp.bfloat16)
@@ -262,8 +263,8 @@
         lane = lax.broadcasted_iota(jnp.int32, gbuf.shape[2:], 1)
         return jnp.where(lax.rem(lax.div(lane, ru), 2) == 0, gbuf[0, s - 1], gbuf[1, s - 1])
 
-    def forward(s):
-        for p in range(pieces_u):
+    def forward(s, first=0, last=pieces_u):
+        for p in range(first, last):
             for d in range(2):
                 u_copy(d, s - 1, p).wait_recv()
                 if s < hops:
@@ -271,37 +272,32 @@
 
     for t in range(3):
         load(t).wait()
+    for s in range(1, hops + 1):
+        for d in range(2):
+            g_copy(d, s).start()
     experts(0, gates_of(0), 0, own)
+    share_out(2, 0)
+    for t in range(3):
+        hand(0, t).wait()
+    collect(0)
+    experts(0, gates_of(0), own, own)
+    forward(1)
+    share_out(2, 1)
     for s in range(1, hops + 1):
         for d in range(2):
-            g_copy(d, s).start()
-    for t in range(3):
-        hand(0, t).wait()
-    share_out(1, 0)
-    forward(1)
-    experts(0, gates_of(0), own, own)
-    share_out(1, 1)
-    for s in range(1, hops + 1):
-        for d in range(2):
             g_copy(d, s).wait()
-    experts(1, gates_of(1), 0, own)
-    share_out(2, 0)
+    experts(1, gates_of(1), 0, 2 * own)
     forward(2)
-    experts(1, gates_of(1), own, own)
-    share_out(2, 1)
-    collect(0)
+    collect(1)
     experts(2, gates_of(2), 0, 2 * own)
-    for s in range(3, hops + 1):
+    for s in range(3, hops):
         forward(s)
-    collect(1)
-    experts(hops, gates_of(hops), 0, 2 * own)
     collect(2)
+    for t in range(3):
+        hand(1, t).wait_recv()
     for p in range(pieces_u):
-        experts(hops, gates_of(hops), 2 * own, own, p * 2 * ru, 2 * ru)
-        if p == 0:
-            for t in range(3):
-                hand(1, t).wait_recv()
-        experts(hops, gates_of(hops), 3 * own, own, p * 2 * ru, 2 * ru)
+        forward(hops, p, p + 1)
+        experts(hops, gates_of(hops), 0, 4 * own, p * 2 * ru, 2 * ru)
         for q in range(p * per, (p + 1) * per):
             for d in range(2):
                 a_copy(d, hops, q).start()
@@ -319,17 +315,11 @@
                     y_ref[rows] = (y_ref[rows].astype(jnp.float32) + (part[s, rows] + acc[s, rows])).astype(y_ref.dtype)
 
 
-    def drain_ring(s, _):
-        for m in range(mats):
-            for d in range(2):
-                across(d, s, m).wait_send()
-
-                @pl.when(s < n - 1)
-                def _():
-                    ring(d, s, m).wait_send()
-        return 0
-
-    lax.fori_loop(0, n, drain_ring, 0)
+    for k in order:
+        across(k).wait_send()
+        if k:
+            along(k).wait_send()
+            each_group(lambda j: outward(k, j).wait_send())
 
     def drain_groups(j, _):
         for t in range(3):
@@ -366,7 +356,7 @@
         in_specs=[vmem, any_spec, any_spec, any_spec, any_spec, vmem, vmem, any_spec, any_spec, any_spec],
         out_specs=vmem,
         scratch_shapes=[
-            pltpu.VMEM((4, dim, dim), bf16),
+            pltpu.VMEM((4, n, 2, w_query.shape[0], dim), bf16),
             pltpu.VMEM((tok, dim), bf16),
             pltpu.VMEM((3, tok, dim), bf16),
             pltpu.VMEM((hops + 1, tok, dim), bf16),
@@ -377,7 +367,7 @@
             pltpu.VMEM((total, dim, ff), bf16),
             pltpu.VMEM((total, dim, ff), bf16),
             pltpu.VMEM((total, ff, dim), bf16),
-            dma((2, n, 4)), dma((2, n, 4)), dma((2, n, 4)), dma((2, n, 4)), dma((4,)), dma((3,)),
+            dma((n,)), dma((n,)), dma((n, groups - 1)), dma((n, groups - 1)), dma((n,)), dma((n,)), dma((4,)), dma((3,)),
             dma((3, 2)), dma((3, 2)), dma((3, 2, groups - 1)), dma((3, 2, groups - 1)), dma((2, 3)), dma((2, 3)),
             dma((2, hops, pieces_u)), dma((2, hops, pieces_u)),
             dma((2, hops, pieces_a)), dma((2, hops, pieces_a)),

time: 262 us -> 230 us (0.88)
  Pallas kernels: 254 us -> 222 us
    pallas_call x1, Pallas kernels: 254 us -> 222 us  [layer(): pl.pallas_call(functools.partial(layer_kernel, n, groups, head_dim, piece...]
where the time goes in v5:
time: 230 us; the launch traced here: 229 us
  Pallas kernels  222 us (97%)
  local copies, waits for them, and re-layouts  7.67 us (3%)
    pallas_call x1, Pallas kernels, layer(): pl.pallas_call(functools.partial(layer_kernel, n, groups, head_dim, piece...  222 us
    reshape x3, local copies, waits for them, and re-layouts, local_layer(): flat = [w.reshape(w.shape[0], -1) for w in (w_query, w_key, w_value)]  5.4 us

profile of v5, /device:TPU:21, one launch (start us, length us, event | category | flops | bytes accessed | tf_op | source)
XLA Modules:
  0.0 229.4 jit_solution(16425304621982780292)
XLA Ops:
  0.0 1.8 reshape.19.wq_hbm
  1.8 1.8 reshape.20.wk_hbm
  3.6 1.8 reshape.21.wv_hbm
  5.4 221.7 %layer_ring.1 = bf16[512,1024]{1,0:T(8,128)(2,1)} custom-call(bf16[512,1024]{1,0:T(8,128)(2,1)} %bitcast.7, bf16[64,1024]{1,0:T(8,128)(2,1)} %reshape.19.wq_hbm, bf16[64,1024]{1,0:T(8,128)(2,1)} %reshape.20.wk_hbm, bf16[64,1024]{1,0:T(8,128)(2,1)} %reshape.21.wv_hbm, bf16[64,1024]{1,0:T(8,128)(2,1)} %wo_hbm.1, f32[32,1024]{1,0:T(8,128)} %bitcast.8, ...), custom_call_target="tpu_custom_call" | custom-call | tf_op jit(solution)/shard_map/layer_ring/pallas_call | solution.py:353
  227.1 2.3 copy.12

commit v6 on v5

--- a/solution.py
+++ b/solution.py
@@ -1,4 +1,5 @@
 import functools
+import math
 
 import jax
 import jax.numpy as jnp
@@ -37,13 +38,13 @@
         c_ref[rows, cols] = context.astype(jnp.bfloat16)
 
 
-def layer_kernel(n, groups, head_dim, x_ref, wq_hbm, wk_hbm, wv_hbm, wo_hbm, wr_ref, ids_ref, e1_hbm, e3_hbm, e2_hbm, y_ref,
+def layer_kernel(n, groups, head_dim, x_ref, wqkv_hbm, wo_hbm, wr_ref, ids_ref, e1_hbm, e3_hbm, e2_hbm, y_ref,
                  wbuf, nbuf, qkv, ubuf, g_own, gbuf, part, acc, w1, w3, w2,
-                 b_send, b_recv, c_send, c_recv, d_send, d_recv, loc, w_loc, z_send, z_recv, s_send, s_recv, w_send, w_recv,
+                 b_send, b_recv, c_send, c_recv, c2_send, c2_recv, d_send, d_recv, loc, w_loc, z_send, z_recv, s_send, s_recv, s2_send, s2_recv, w_send, w_recv,
                  u_send, u_recv, a_send, a_recv, g_send, g_recv, *, pieces_u, pieces_a):
     me, group = lax.axis_index('ep'), lax.axis_index('dp')
     pos, core = lax.div(me, 2), lax.rem(me, 2)
-    share = wq_hbm.shape[0]
+    share = wo_hbm.shape[0]
     mats = wbuf.shape[0]
     tok, dim = x_ref.shape
     own, classes = e1_hbm.shape[0], g_own.shape[0]
@@ -55,8 +56,53 @@
     def peer(z):
         return {'ep': lax.rem(z, n) * 2 + core}
 
-    def other(j):
-        return {'dp': lax.rem(group + j, groups)}
+
+    low = math.isqrt(groups) if math.isqrt(groups) ** 2 == groups else groups
+    sides = (low, groups // low)
+    spots = (lax.rem(group, low), lax.div(group, low))
+
+    def member(f, i, j):
+        at = [0, 0]
+        at[f] = lax.rem(spots[f] + i + sides[f], sides[f])
+        at[1 - f] = lax.rem(spots[1 - f] + j + sides[1 - f], sides[1 - f])
+        return at[1] * low + at[0]
+
+    def swap_first(f, piece, sems, i):
+        return remote(piece(group), piece(group), sems[0].at[i - 1], sems[1].at[i - 1], {'dp': member(f, i, 0)})
+
+    def swap_then(f, piece, sems, i, j):
+        ref, at = piece(member(f, -i, 0)), i * (sides[1 - f] - 1) + j - 1
+        return remote(ref, ref, sems[2].at[at], sems[3].at[at], {'dp': member(f, 0, j)})
+
+    def firsts(f):
+        return range(1, sides[f])
+
+    def thens(f):
+        return range(1, sides[1 - f])
+
+    def swap_start(f, piece, sems):
+        for i in firsts(f):
+            swap_first(f, piece, sems, i).start()
+        for j in thens(f):
+            swap_then(f, piece, sems, 0, j).start()
+
+    def swap_relay(f, piece, sems):
+        for i in firsts(f):
+            swap_first(f, piece, sems, i).wait_recv()
+            for j in thens(f):
+                swap_then(f, piece, sems, i, j).start()
+
+    def swap_take(f, piece, sems):
+        for i in range(sides[f]):
+            for j in thens(f):
+                swap_then(f, piece, sems, i, j).wait_recv()
+
+    def swap_drain(f, piece, sems):
+        for i in firsts(f):
+            swap_first(f, piece, sems, i).wait_send()
+        for i in range(sides[f]):
+            for j in thens(f):
+                swap_then(f, piece, sems, i, j).wait_send()
 
     sibling = {'ep': pos * 2 + (1 - core)}
 
@@ -70,7 +116,7 @@
         return 0
 
     def greet_groups(j, _):
-        pl.semaphore_signal(barrier, inc=1, device_id=other(j), device_id_type=MESH)
+        pl.semaphore_signal(barrier, inc=1, device_id={'dp': lax.rem(group + j, groups)}, device_id_type=MESH)
         return 0
 
     lax.fori_loop(1, n, greet_ring, 0)
@@ -79,37 +125,30 @@
 
 
     parts, whole = max(1, groups // mats), max(1, mats // groups)
-    first_mat, first_row = lax.div(group * mats, groups), lax.rem(group, parts) * (share // parts)
     order = sorted(range(n), key=lambda k: min(k, n - k))
 
-    def piece(k):
-        return wbuf.at[pl.ds(first_mat, whole), lax.rem(pos + n - k, n), core, pl.ds(pl.multiple_of(first_row, share // parts), share // parts)]
+    def shard_piece(k, g):
+        row = pl.multiple_of(lax.rem(g, parts) * (share // parts), share // parts)
+        return wbuf.at[pl.ds(lax.div(g * mats, groups), whole), lax.rem(pos + n - k, n), core, pl.ds(row, share // parts)]
 
     def along(k):
-        return remote(piece(0), piece(0), b_send.at[k], b_recv.at[k], peer(pos + k))
-
-    def outward(k, j):
-        return remote(piece(k), piece(k), c_send.at[k, j - 1], c_recv.at[k, j - 1], other(j))
+        return remote(shard_piece(0, group), shard_piece(0, group), b_send.at[k], b_recv.at[k], peer(pos + k))
+
+    def outward(k):
+        return k % 2, functools.partial(shard_piece, k), [r.at[k] for r in (c_send, c_recv, c2_send, c2_recv)]
 
     def across(k):
         block = wbuf.at[:, lax.rem(pos + n - k, n), core]
         return remote(block, block, d_send.at[k], d_recv.at[k], sibling)
 
-    def each_group(do):
-        def step(j, _):
-            do(j)
-            return 0
-
-        lax.fori_loop(1, groups, step, 0)
-
 
     near, away = lax.div(pos, classes) * 2 * own, (1 - lax.div(pos, classes)) * 2 * own
     base = [near + core * own, near + (1 - core) * own, away + core * own, away + (1 - core) * own]
     experts_of = ((e1_hbm, w1), (e3_hbm, w3), (e2_hbm, w2))
 
-    def rows_of(t, d):
+    def rows_of(t, d, g):
         size = experts_of[t][0].shape[1] // (2 * groups)
-        return pl.ds(pl.multiple_of((group * 2 + d) * size, size), size)
+        return pl.ds(pl.multiple_of((g * 2 + d) * size, size), size)
 
     def load(t):
         return pltpu.make_async_copy(experts_of[t][0], experts_of[t][1].at[pl.ds(base[0], own)], w_loc.at[t])
@@ -119,33 +158,29 @@
         return remote(experts_of[t][0] if r == 0 else kept, kept, w_send.at[r, t], w_recv.at[r, t], sibling)
 
     def fetch(t, d):
-        rows = rows_of(t, d)
+        rows = rows_of(t, d, group)
         return remote(experts_of[t][0].at[:, rows], experts_of[t][1].at[pl.ds(base[0], own), rows], z_send.at[t, d], z_recv.at[t, d], peer(pos + n // 2))
 
-    def spread(t, d, j):
-        piece = experts_of[t][1].at[pl.ds(base[2], own), rows_of(t, d)]
-        return remote(piece, piece, s_send.at[t, d, j - 1], s_recv.at[t, d, j - 1], other(j))
+    def spread(t, d):
+        def expert_piece(g):
+            return experts_of[t][1].at[pl.ds(base[2], own), rows_of(t, d, g)]
+
+        return d, expert_piece, [r.at[t, d] for r in (s_send, s_recv, s2_send, s2_recv)]
 
     def share_out(t, d):
         fetch(t, d).wait_recv()
-
-        def send(j, _):
-            spread(t, d, j).start()
-            return 0
-
-        lax.fori_loop(1, groups, send, 0)
+        swap_start(*spread(t, d))
+
+    def share_on(t, d):
+        swap_relay(*spread(t, d))
 
     def collect(t):
-        def take(j, _):
-            for d in range(2):
-                spread(t, d, j).wait_recv()
-            return 0
-
-        lax.fori_loop(1, groups, take, 0)
+        for d in range(2):
+            swap_take(*spread(t, d))
         hand(1, t).start()
 
     shards = []
-    for m, src in enumerate((wq_hbm, wk_hbm, wv_hbm, wo_hbm)):
+    for m, src in enumerate((wqkv_hbm.at[0], wqkv_hbm.at[1], wqkv_hbm.at[2], wo_hbm)):
         shards.append(pltpu.make_async_copy(src, wbuf.at[m, pos, core], loc.at[m]))
         shards[-1].start()
     for t in range(3):
@@ -156,23 +191,26 @@
     for k in order[1:]:
         along(k).start()
     for t in range(3):
-        for d in range(2):
-            fetch(t, d).start()
-    for t in range(3):
         hand(0, t).start()
     nbuf[...] = rms_norm(x_ref[...]).astype(jnp.bfloat16)
     for s in range(hops + 1):
         part[s] = jnp.zeros(part.shape[1:], jnp.float32)
 
+    across(0).start()
+    for i in range(n + 1):
+        if i + 1 < n:
+            along(order[i + 1]).wait_recv()
+            swap_start(*outward(order[i + 1]))
+        if i == n // 2 - 1:
+            for t in range(3):
+                for d in range(2):
+                    fetch(t, d).start()
+        if i > 1:
+            swap_relay(*outward(order[i - 1]))
+    share_out(0, 0)
     for k in order[1:]:
-        along(k).wait_recv()
-        each_group(lambda j: outward(k, j).start())
-    across(0).start()
-    for k in order[1:]:
-        each_group(lambda j: outward(k, j).wait_recv())
+        swap_take(*outward(k))
         across(k).start()
-    share_out(0, 0)
-    share_out(0, 1)
     for k in order:
         across(k).wait_recv()
     width = dim // 2
@@ -184,6 +222,8 @@
         return 0
 
     lax.fori_loop(0, 6, project, 0)
+    share_out(0, 1)
+    share_on(0, 0)
     pairs = dim // 128
 
     def heads(i, _):
@@ -191,18 +231,20 @@
 
         @pl.when(i == pairs // 4)
         def _():
+            share_on(0, 1)
+
+        @pl.when(i == 5 * pairs // 8)
+        def _():
             share_out(1, 0)
-
-        @pl.when(i == 3 * pairs // 4)
-        def _():
-            share_out(1, 1)
         return 0
 
     lax.fori_loop(0, pairs, heads, 0)
+    share_on(1, 0)
     for j in range(2):
         cols = slice(j * width, (j + 1) * width)
         mixed = jnp.dot(nbuf[...], wbuf[3, :, :, :, cols].reshape(dim, width), preferred_element_type=jnp.float32)
         y_ref[:, cols] = (x_ref[:, cols].astype(jnp.float32) + mixed).astype(jnp.bfloat16)
+    share_out(1, 1)
     z = rms_norm(y_ref[...])
     ubuf[0] = z.astype(jnp.bfloat16)
     logits = lax.dot_general(wr_ref[...], z, (((1,), (1,)), ((), ())), precision=lax.Precision.HIGHEST, preferred_element_type=jnp.float32)
@@ -275,24 +317,28 @@
     for s in range(1, hops + 1):
         for d in range(2):
             g_copy(d, s).start()
+    share_on(1, 1)
+    share_out(2, 0)
     experts(0, gates_of(0), 0, own)
-    share_out(2, 0)
     for t in range(3):
         hand(0, t).wait()
     collect(0)
     experts(0, gates_of(0), own, own)
+    share_on(2, 0)
+    share_out(2, 1)
     forward(1)
-    share_out(2, 1)
     for s in range(1, hops + 1):
         for d in range(2):
             g_copy(d, s).wait()
-    experts(1, gates_of(1), 0, 2 * own)
+    experts(1, gates_of(1), 0, own)
+    share_on(2, 1)
+    collect(1)
+    experts(1, gates_of(1), own, own)
     forward(2)
-    collect(1)
+    collect(2)
     experts(2, gates_of(2), 0, 2 * own)
     for s in range(3, hops):
         forward(s)
-    collect(2)
     for t in range(3):
         hand(1, t).wait_recv()
     for p in range(pieces_u):
@@ -319,15 +365,11 @@
         across(k).wait_send()
         if k:
             along(k).wait_send()
-            each_group(lambda j: outward(k, j).wait_send())
-
-    def drain_groups(j, _):
-        for t in range(3):
-            for d in range(2):
-                spread(t, d, j).wait_send()
-        return 0
-
-    lax.fori_loop(1, groups, drain_groups, 0)
+            swap_drain(*outward(k))
+
+    for t in range(3):
+        for d in range(2):
+            swap_drain(*spread(t, d))
     for t in range(3):
         hand(1, t).wait_send()
         for d in range(2):
@@ -340,7 +382,7 @@
                 a_copy(d, s + 1, p).wait_send()
 
 
-def layer(x, w_query, w_key, w_value, w_out, w_router_t, ids_t, w_one, w_three, w_two, n, groups, head_dim):
+def layer(x, w_qkv, w_out, w_router_t, ids_t, w_one, w_three, w_two, n, groups, head_dim):
     tok, dim = x.shape
     own, _, ff = w_one.shape
     classes = n // 2
@@ -353,10 +395,10 @@
     return pl.pallas_call(
         functools.partial(layer_kernel, n, groups, head_dim, pieces_u=pieces_u, pieces_a=pieces_a),
         out_shape=jax.ShapeDtypeStruct((tok, dim), bf16),
-        in_specs=[vmem, any_spec, any_spec, any_spec, any_spec, vmem, vmem, any_spec, any_spec, any_spec],
+        in_specs=[vmem, any_spec, any_spec, vmem, vmem, any_spec, any_spec, any_spec],
         out_specs=vmem,
         scratch_shapes=[
-            pltpu.VMEM((4, n, 2, w_query.shape[0], dim), bf16),
+            pltpu.VMEM((4, n, 2, w_out.shape[0], dim), bf16),
             pltpu.VMEM((tok, dim), bf16),
             pltpu.VMEM((3, tok, dim), bf16),
             pltpu.VMEM((hops + 1, tok, dim), bf16),
@@ -367,15 +409,15 @@
             pltpu.VMEM((total, dim, ff), bf16),
             pltpu.VMEM((total, dim, ff), bf16),
             pltpu.VMEM((total, ff, dim), bf16),
-            dma((n,)), dma((n,)), dma((n, groups - 1)), dma((n, groups - 1)), dma((n,)), dma((n,)), dma((4,)), dma((3,)),
-            dma((3, 2)), dma((3, 2)), dma((3, 2, groups - 1)), dma((3, 2, groups - 1)), dma((2, 3)), dma((2, 3)),
+            dma((n,)), dma((n,)), *(dma((n, groups)) for _ in range(4)), dma((n,)), dma((n,)), dma((4,)), dma((3,)),
+            dma((3, 2)), dma((3, 2)), *(dma((3, 2, groups)) for _ in range(4)), dma((2, 3)), dma((2, 3)),
             dma((2, hops, pieces_u)), dma((2, hops, pieces_u)),
             dma((2, hops, pieces_a)), dma((2, hops, pieces_a)),
             dma((2, hops)), dma((2, hops)),
         ],
         compiler_params=pltpu.CompilerParams(collective_id=1, has_side_effects=True, vmem_limit_bytes=67_000_000),
         name='layer_ring',
-    )(x, w_query, w_key, w_value, w_out, w_router_t, ids_t, w_one, w_three, w_two)
+    )(x, w_qkv, w_out, w_router_t, ids_t, w_one, w_three, w_two)
 
 
 def solution(mesh):
@@ -386,9 +428,9 @@
 
     def local_layer(tokens, w_query, w_key, w_value, w_out, w_router, w_one, w_three, w_two, expert_ids):
         tok, dim = tokens.shape[0] * tokens.shape[1], tokens.shape[2]
-        flat = [w.reshape(w.shape[0], -1) for w in (w_query, w_key, w_value)]
+        flat = jnp.stack([w_query, w_key, w_value]).reshape(3, w_query.shape[0], -1)
         ids_t = expert_ids.reshape(tok, -1).T
-        out = layer(tokens.reshape(tok, dim), *flat, w_out, w_router.T, ids_t, w_one, w_three, w_two, n, groups, w_query.shape[2])
+        out = layer(tokens.reshape(tok, dim), flat, w_out, w_router.T, ids_t, w_one, w_three, w_two, n, groups, w_query.shape[2])
         return out.reshape(tokens.shape)
 
     return jax.shard_map(local_layer, mesh=mesh, in_specs=(tok_spec, row_spec, row_spec, row_spec, row_spec, P(), row_spec, row_spec, row_spec, tok_spec), out_specs=tok_spec, check_vma=False)

time: 230 us -> 225 us (0.978)
  Pallas kernels: 222 us -> 217 us
    reshape x3 -> x0, local copies, waits for them, and re-layouts: 5.4 us -> none  [local_layer(): flat = [w.reshape(w.shape[0], -1) for w in (w_query, w_key, w_value)]]
    pallas_call x1, Pallas kernels: 222 us -> 217 us  [layer(): pl.pallas_call(functools.partial(layer_kernel, n, groups, head_dim, piece...]
    another operation x0 -> x3, local copies, waits for them, and re-layouts: none -> 3.44 us  [local_layer(): flat = jnp.stack([w_query, w_key, w_value]).reshape(3, w_query.shape[0], -1)]
where the time goes in v6:
time: 225 us; the launch traced here: 224 us
  Pallas kernels  217 us (96%)
  local copies, waits for them, and re-layouts  5.7 us (3%)
    pallas_call x1, Pallas kernels, layer(): pl.pallas_call(functools.partial(layer_kernel, n, groups, head_dim, piece...  217 us

profile of v6, /device:TPU:21, one launch (start us, length us, event | category | flops | bytes accessed | tf_op | source)
XLA Modules:
  0.0 223.9 jit_solution(17675772832736152241)
XLA Ops:
  0.0 1.1 stack.12
  1.2 1.1 stack.13
  2.3 1.1 stack.14
  3.5 0.8 pad_maximum_fusion.wqkv_hbm
  4.3 217.4 %layer_ring.1 = bf16[512,1024]{1,0:T(8,128)(2,1)} custom-call(bf16[512,1024]{1,0:T(8,128)(2,1)} %bitcast.7, bf16[3,64,1024]{2,1,0:T(8,128)(2,1)} %pad_maximum_fusion.wqkv_hbm, bf16[64,1024]{1,0:T(8,128)(2,1)} %wo_hbm.1, f32[32,1024]{1,0:T(8,128)} %bitcast.8, s32[8,512]{1,0:T(8,128)} %bitcast.9, bf16[2,1024,512]{2,1,0:T(8,128)(2,1)} %e1_hbm.1, ...), custom_call_target="tpu_custom_call" | custom-call | tf_op jit(solution)/shard_map/layer_ring/pallas_call | solution.py:395
  221.6 2.3 %copy.12 = bf16[1,512,1024]{2,1,0:T(8,128)(2,1)} copy(bf16[1,512,1024]{2,1,0:T(8,128)(2,1)} %bitcast.6) | data formatting | bytes 2097152

commit v7 on v6

--- a/solution.py
+++ b/solution.py
@@ -335,15 +335,17 @@
     collect(1)
     experts(1, gates_of(1), own, own)
     forward(2)
+    experts(2, gates_of(2), 0, 2 * own)
     collect(2)
-    experts(2, gates_of(2), 0, 2 * own)
     for s in range(3, hops):
         forward(s)
+    for p in range(pieces_u):
+        forward(hops, p, p + 1)
+        experts(hops, gates_of(hops), 0, 2 * own, p * 2 * ru, 2 * ru)
     for t in range(3):
         hand(1, t).wait_recv()
     for p in range(pieces_u):
-        forward(hops, p, p + 1)
-        experts(hops, gates_of(hops), 0, 4 * own, p * 2 * ru, 2 * ru)
+        experts(hops, gates_of(hops), 2 * own, 2 * own, p * 2 * ru, 2 * ru)
         for q in range(p * per, (p + 1) * per):
             for d in range(2):
                 a_copy(d, hops, q).start()

time: 225 us -> 230 us (1.022)
  Pallas kernels: 217 us -> 223 us
    pallas_call x1, Pallas kernels: 217 us -> 223 us  [layer(): pl.pallas_call(functools.partial(layer_kernel, n, groups, head_dim, piece...]
where the time goes in v7:
time: 230 us
  Pallas kernels  223 us (97%)
  local copies, waits for them, and re-layouts  5.7 us (2%)
    pallas_call x1, Pallas kernels, layer(): pl.pallas_call(functools.partial(layer_kernel, n, groups, head_dim, piece...  223 us

profile of v7, /device:TPU:21, one launch (start us, length us, event | category | flops | bytes accessed | tf_op | source)
XLA Modules:
  0.0 229.7 jit_solution(8675196138186665777)
XLA Ops:
  0.0 1.1 stack.12
  1.2 1.1 stack.13
  2.3 1.1 stack.14
  3.5 0.8 pad_maximum_fusion.wqkv_hbm
  4.3 223.2 %layer_ring.1 = bf16[512,1024]{1,0:T(8,128)(2,1)} custom-call(bf16[512,1024]{1,0:T(8,128)(2,1)} %bitcast.7, bf16[3,64,1024]{2,1,0:T(8,128)(2,1)} %pad_maximum_fusion.wqkv_hbm, bf16[64,1024]{1,0:T(8,128)(2,1)} %wo_hbm.1, f32[32,1024]{1,0:T(8,128)} %bitcast.8, s32[8,512]{1,0:T(8,128)} %bitcast.9, bf16[2,1024,512]{2,1,0:T(8,128)(2,1)} %e1_hbm.1, ...), custom_call_target="tpu_custom_call" | custom-call | tf_op jit(solution)/shard_map/layer_ring/pallas_call | solution.py:397
  227.4 2.3 copy.12
